TPU v7x, 128 devices: a whole 4x4x4 slice. The times are simulated.
128 devices in a mesh: batch: 1, row: 16 (over z, y), col: 8 (over x, core).
Axes of the slice: x: 4, y: 4, z: 4, core: 2. Of those that a mesh axis runs over, the one named last changes fastest.
Arguments:
- lower_tri: bfloat16 [16384, 16384], P(('batch', 'row'), 'col')
- right_side: bfloat16 [16384, 4096], P(('batch', 'row'), 'col')
- grad_out: bfloat16 [16384, 4096], P(('batch', 'row'), 'col')
Outputs:
- output 1: bfloat16 [16384, 4096], P(('batch', 'row'), 'col')
- output 2: bfloat16 [16384, 16384], P(('batch', 'row'), 'col')
All inputs are finite; a program needn't handle non-finite values.
Results may differ from a plain program's by a relative error of at most 0.001.
Values are sent between devices in bfloat16 or wider.
A program may use at most 1 GiB of HBM per device.

v0:
```python
import jax
import jax.numpy as jnp
from jax import lax
from jax.sharding import PartitionSpec as P

BLOCK_SIZE = 256


def solution(mesh):
    mesh_rows = mesh.shape["row"]
    mesh_cols = mesh.shape["col"]
    group_size = max(mesh_rows, mesh_cols)
    row_step = group_size // mesh_rows
    col_step = group_size // mesh_cols
    block_spec = P(("batch", "row"), "col")

    def per_device(lower_tri, right_side, grad_out):
        rows_here, cols_here = lower_tri.shape
        num_cols = right_side.shape[1]
        num_steps = rows_here // (row_step * BLOCK_SIZE)
        right_pieces = []
        lower_pieces = []
        for step_idx in range(num_steps):
            first_row = step_idx * row_step * BLOCK_SIZE
            left_rows = rows_here - first_row
            grad_rows = grad_out[first_row:]
            lower_panel = lower_tri[first_row:, step_idx * col_step * BLOCK_SIZE:(step_idx + 1) * col_step * BLOCK_SIZE]
            gathered = lax.all_gather(lower_panel.reshape(left_rows, col_step, BLOCK_SIZE), "col", axis=2)
            right_part = jnp.einsum("rbqe,rf->bqef", gathered, grad_rows, preferred_element_type=jnp.float32)
            right_mine = lax.psum_scatter(right_part.reshape(row_step, mesh_rows * BLOCK_SIZE, num_cols), "row", scatter_dimension=1, tiled=True)
            right_pieces.append(right_mine.reshape(row_step * BLOCK_SIZE, num_cols).astype(jnp.bfloat16))
            side_block = right_side[first_row:first_row + row_step * BLOCK_SIZE].reshape(row_step, BLOCK_SIZE, num_cols)
            side_rows = lax.all_gather(side_block, "row", axis=1).reshape(col_step, mesh_cols, BLOCK_SIZE, num_cols)
            lower_part = jnp.einsum("rf,bqef->rbqe", grad_rows, side_rows, preferred_element_type=jnp.float32)
            lower_mine = lax.psum_scatter(lower_part.reshape(left_rows, col_step, mesh_cols * BLOCK_SIZE), "col", scatter_dimension=2, tiled=True)
            lower_piece = lower_mine.reshape(left_rows, col_step * BLOCK_SIZE).astype(jnp.bfloat16)
            lower_pieces.append(jnp.pad(lower_piece, ((first_row, 0), (0, 0))))
        grad_right = jnp.concatenate(right_pieces, axis=0)
        grad_lower = jnp.concatenate(lower_pieces, axis=1)
        row_pos = jnp.arange(rows_here)[:, None]
        col_pos = jnp.arange(cols_here)[None, :]
        row_global = (row_pos // BLOCK_SIZE * mesh_rows + lax.axis_index("row")) * BLOCK_SIZE + row_pos % BLOCK_SIZE
        col_global = (col_pos // BLOCK_SIZE * mesh_cols + lax.axis_index("col")) * BLOCK_SIZE + col_pos % BLOCK_SIZE
        grad_lower = jnp.where(row_global >= col_global, grad_lower, 0.0).astype(jnp.bfloat16)
        return grad_right, grad_lower

    return jax.shard_map(per_device, mesh=mesh, in_specs=(block_spec, block_spec, block_spec), out_specs=(block_spec, block_spec), check_vma=False)
```

profile of v0, /device:TPU:1, one launch (start us, length us, event | category | flops | bytes accessed | tf_op | source)
XLA Modules:
  0.0 1025.8 jit_solution(2076390476470572772)
XLA Ops:
  19.6 45.3 %all-gather.27.cloned.1.call-done = bf16[4096,512]{1,0:T(8,128)(2,1)} async-done(((bf16[256,512]{1,0:T(8,128)(2,1)}), bf16[4096,512]{1,0:T(8,128)(2,1)}) %all-gather.27.cloned.1.call-update) | async-done | bytes 4194320 | tf_op jit(solution)/shard_map/all_gather | solution.py:33
  70.4 21.4 %all-gather.19.cloned.1.call-done = bf16[256,2,8,256]{0,3,2,1:T(8,128)(2,1)} async-done(((bf16[256,2,1,256]{0,3,2,1:T(8,128)(2,1)}), bf16[256,2,8,256]{0,3,2,1:T(8,128)(2,1)}) %all-gather.19.cloned.1.call-update) | async-done | bytes 2097168 | tf_op jit(solution)/shard_map/all_gather | solution.py:28
  98.1 27.9 %all-gather.17.cloned.1.call-done = bf16[512,2,8,256]{0,3,2,1:T(8,128)(2,1)} async-done(((bf16[512,2,1,256]{0,3,2,1:T(8,128)(2,1)}), bf16[512,2,8,256]{0,3,2,1:T(8,128)(2,1)}) %all-gather.17.cloned.1.call-update) | async-done | bytes 4194320 | tf_op jit(solution)/shard_map/all_gather | solution.py:28
  126.0 7.7 fusion.18
  133.8 44.7 %all-gather.25.cloned.1.call-done = bf16[4096,512]{1,0:T(8,128)(2,1)} async-done(((bf16[256,512]{1,0:T(8,128)(2,1)}), bf16[4096,512]{1,0:T(8,128)(2,1)}) %all-gather.25.cloned.1.call-update) | async-done | bytes 4194320 | tf_op jit(solution)/shard_map/all_gather | solution.py:33
  178.5 7.9 fusion.20
  186.5 34.4 %all-gather.15.cloned.1.call-done = bf16[768,2,8,256]{0,3,2,1:T(8,128)(2,1)} async-done(((bf16[768,2,1,256]{0,3,2,1:T(8,128)(2,1)}), bf16[768,2,8,256]{0,3,2,1:T(8,128)(2,1)}) %all-gather.15.cloned.1.call-update) | async-done | bytes 6291472 | tf_op jit(solution)/shard_map/all_gather | solution.py:28
  220.9 8.5 fusion.12
  229.4 43.3 %all-gather.13.cloned.1.call-done = bf16[1024,2,8,256]{0,3,2,1:T(8,128)(2,1)} async-done(((bf16[1024,2,1,256]{0,3,2,1:T(8,128)(2,1)}), bf16[1024,2,8,256]{0,3,2,1:T(8,128)(2,1)}) %all-gather.13.cloned.1.call-update) | async-done | bytes 8388624 | tf_op jit(solution)/shard_map/all_gather | solution.py:28
  272.7 10.2 fusion.8
  283.2 42.5 %all-gather.23.cloned.1.call-done = bf16[4096,512]{1,0:T(8,128)(2,1)} async-done(((bf16[256,512]{1,0:T(8,128)(2,1)}), bf16[4096,512]{1,0:T(8,128)(2,1)}) %all-gather.23.cloned.1.call-update) | async-done | bytes 4194320 | tf_op jit(solution)/shard_map/all_gather | solution.py:33
  325.7 8.6 fusion.14
  334.3 44.3 %all-gather.21.cloned.1.call-done = bf16[4096,512]{1,0:T(8,128)(2,1)} async-done(((bf16[256,512]{1,0:T(8,128)(2,1)}), bf16[4096,512]{1,0:T(8,128)(2,1)}) %all-gather.21.cloned.1.call-update) | async-done | bytes 4194320 | tf_op jit(solution)/shard_map/all_gather | solution.py:33
  378.6 10.3 %fusion.10 = f32[1024,2,2048]{2,0,1:T(8,128)} fusion(bf16[2,2048,512]{2,1,0:T(8,128)(2,1)} %bitcast.78, bf16[1024,512]{1,0:T(8,128)(2,1)S(1)} %copy-done), kind=kOutput, calls=%fused_computation.17 | convolution fusion | flops 4294967296 | bytes 22020096 | tf_op jit(solution)/shard_map/rf,bqef->rbqe/dot_general | solution.py:34
  389.0 27.5 %reduce-scatter.23.cloned.1.call-done = f32[256,2,256]{2,0,1:T(8,128)} async-done(((f32[256,2,2048]{2,0,1:T(8,128)}), f32[256,2,256]{2,0,1:T(8,128)}) %reduce-scatter.23.cloned.1.call-update) | async-done | bytes 524304 | tf_op jit(solution)/shard_map/reduce_scatter | solution.py:35
  418.4 87.1 %reduce-scatter.15.cloned.1.call-done = f32[1,256,512]{2,1,0:T(8,128)} async-done(((f32[1,4096,512]{2,1,0:T(8,128)}), f32[1,256,512]{2,1,0:T(8,128)}) %reduce-scatter.15.cloned.1.call-update) | async-done | bytes 524304 | tf_op jit(solution)/shard_map/reduce_scatter | solution.py:30
  506.6 87.2 %reduce-scatter.13.cloned.1.call-done = f32[1,256,512]{2,1,0:T(8,128)} async-done(((f32[1,4096,512]{2,1,0:T(8,128)}), f32[1,256,512]{2,1,0:T(8,128)}) %reduce-scatter.13.cloned.1.call-update) | async-done | bytes 524304 | tf_op jit(solution)/shard_map/reduce_scatter | solution.py:30
  594.9 54.1 %reduce-scatter.21.cloned.1.call-done = f32[512,2,256]{2,0,1:T(8,128)} async-done(((f32[512,2,2048]{2,0,1:T(8,128)}), f32[512,2,256]{2,0,1:T(8,128)}) %reduce-scatter.21.cloned.1.call-update) | async-done | bytes 1048592 | tf_op jit(solution)/shard_map/reduce_scatter | solution.py:35
  650.5 86.2 %reduce-scatter.11.cloned.1.call-done = f32[1,256,512]{2,1,0:T(8,128)} async-done(((f32[1,4096,512]{2,1,0:T(8,128)}), f32[1,256,512]{2,1,0:T(8,128)}) %reduce-scatter.11.cloned.1.call-update) | async-done | bytes 524304 | tf_op jit(solution)/shard_map/reduce_scatter | solution.py:30
  737.7 87.0 %reduce-scatter.9.cloned.1.call-done = f32[1,256,512]{2,1,0:T(8,128)} async-done(((f32[1,4096,512]{2,1,0:T(8,128)}), f32[1,256,512]{2,1,0:T(8,128)}) %reduce-scatter.9.cloned.1.call-update) | async-done | bytes 524304 | tf_op jit(solution)/shard_map/reduce_scatter | solution.py:30
  826.9 73.0 %reduce-scatter.19.cloned.1.call-done = f32[768,2,256]{2,0,1:T(8,128)} async-done(((f32[768,2,2048]{2,0,1:T(8,128)}), f32[768,2,256]{2,0,1:T(8,128)}) %reduce-scatter.19.cloned.1.call-update) | async-done | bytes 1572880 | tf_op jit(solution)/shard_map/reduce_scatter | solution.py:35
  901.6 92.1 %reduce-scatter.17.cloned.1.call-done = f32[1024,2,256]{2,0,1:T(8,128)} async-done(((f32[1024,2,2048]{2,0,1:T(8,128)}), f32[1024,2,256]{2,0,1:T(8,128)}) %reduce-scatter.17.cloned.1.call-update) | async-done | bytes 2097168 | tf_op jit(solution)/shard_map/reduce_scatter | solution.py:35
  996.0 16.9 %compare_select_fusion = bf16[1024,2048]{0,1:T(8,128)(2,1)} fusion(bf16[256,512]{0,1:T(8,128)(2,1)} %bitcast.76, bf16[512,512]{0,1:T(8,128)(2,1)S(1)} %bitcast.74, bf16[768,512]{0,1:T(8,128)(2,1)S(1)} %bitcast.73, bf16[1024,512]{0,1:T(8,128)(2,1)S(1)} %bitcast.71, s32[1024]{0:T(1024)S(1)} %fusion.50, s32[2048]{0:T(1024)S(1)} %fusion.39), kind=kLoop, calls=%fused_computation.10 | loop fusion | flops 41943040 | bytes 6828032 | tf_op jit(solution)/shard_map/jit(_where)/select_n | solution.py:44
  1012.9 6.4 copy.17
  (61 shorter events, 37.2 us)
Async XLA Ops:
  7.2 57.7 %all-gather.27.cloned.1.call-start = ((), (), s32[]{:S(2)}) async-start(), calls=%async_computation.23 | async-start | bytes 4456448 | tf_op jit(solution)/shard_map/all_gather | solution.py:33
  9.4 82.4 %all-gather.19.cloned.1.call-start = ((), (), s32[]{:S(2)}) async-start(), calls=%async_computation.14 | async-start | bytes 2359296 | tf_op jit(solution)/shard_map/all_gather | solution.py:28
  11.3 114.7 %all-gather.17.cloned.1.call-start = ((), (), s32[]{:S(2)}) async-start(), calls=%async_computation.12 | async-start | bytes 4718592 | tf_op jit(solution)/shard_map/all_gather | solution.py:28
  12.5 4.2 slice-start
  13.6 165.0 %all-gather.25.cloned.1.call-start = ((), (), s32[]{:S(2)}) async-start(), calls=%async_computation.22 | async-start | bytes 4456448 | tf_op jit(solution)/shard_map/all_gather | solution.py:33
  14.1 206.7 %all-gather.15.cloned.1.call-start = ((), (), s32[]{:S(2)}) async-start(), calls=%async_computation.10 | async-start | bytes 7077888 | tf_op jit(solution)/shard_map/all_gather | solution.py:28
  15.4 49.5 %copy-start = (bf16[1024,512]{1,0:T(8,128)(2,1)S(1)}, bf16[1024,512]{1,0:T(8,128)(2,1)}, u32[]{:S(2)}) copy-start(bf16[1024,512]{1,0:T(8,128)(2,1)} %param.5) | copy-start | bytes 3145732
  16.6 256.1 %all-gather.13.cloned.1.call-start = ((), (), s32[]{:S(2)}) async-start(), calls=%async_computation.8 | async-start | bytes 9437184 | tf_op jit(solution)/shard_map/all_gather | solution.py:28
  18.0 307.7 %all-gather.23.cloned.1.call-start = ((), (), s32[]{:S(2)}) async-start(), calls=%async_computation.21 | async-start | bytes 4456448 | tf_op jit(solution)/shard_map/all_gather | solution.py:33
  18.8 359.9 %all-gather.21.cloned.1.call-start = ((), (), s32[]{:S(2)}) async-start(), calls=%async_computation.20 | async-start | bytes 4456448 | tf_op jit(solution)/shard_map/all_gather | solution.py:33
  19.5 396.9 %reduce-scatter.23.cloned.1.call-start = ((), (), s32[]{:S(2)}) async-start(), calls=%async_computation.19 | async-start | bytes 4718592 | tf_op jit(solution)/shard_map/reduce_scatter | solution.py:35
  70.4 435.1 %reduce-scatter.15.cloned.1.call-start = ((), (), s32[]{:S(2)}) async-start(), calls=%async_computation.15 | async-start | bytes 8912896 | tf_op jit(solution)/shard_map/reduce_scatter | solution.py:30
  98.0 495.7 %reduce-scatter.13.cloned.1.call-start = ((), (), s32[]{:S(2)}) async-start(), calls=%async_computation.13 | async-start | bytes 8912896 | tf_op jit(solution)/shard_map/reduce_scatter | solution.py:30
  133.7 515.2 %reduce-scatter.21.cloned.1.call-start = ((), (), s32[]{:S(2)}) async-start(), calls=%async_computation.18 | async-start | bytes 9437184 | tf_op jit(solution)/shard_map/reduce_scatter | solution.py:35
  186.4 550.2 %reduce-scatter.11.cloned.1.call-start = ((), (), s32[]{:S(2)}) async-start(), calls=%async_computation.11 | async-start | bytes 8912896 | tf_op jit(solution)/shard_map/reduce_scatter | solution.py:30
  229.4 595.4 %reduce-scatter.9.cloned.1.call-start = ((), (), s32[]{:S(2)}) async-start(), calls=%async_computation.9 | async-start | bytes 8912896 | tf_op jit(solution)/shard_map/reduce_scatter | solution.py:30
  282.9 617.0 %reduce-scatter.19.cloned.1.call-start = ((), (), s32[]{:S(2)}) async-start(), calls=%async_computation.17 | async-start | bytes 14155776 | tf_op jit(solution)/shard_map/reduce_scatter | solution.py:35
  334.3 659.5 %reduce-scatter.17.cloned.1.call-start = ((), (), s32[]{:S(2)}) async-start(), calls=%async_computation.16 | async-start | bytes 18874368 | tf_op jit(solution)/shard_map/reduce_scatter | solution.py:35
Sparse Core Ops, SparseCore 0:
  10.7 54.1 all-gather.26
  66.6 25.2 all-gather.18
  93.5 32.4 all-gather.16
  128.0 50.4 all-gather.24
  180.1 40.7 all-gather.14
  223.0 49.6 all-gather.12
  274.8 50.8 all-gather.22
  327.8 50.7 all-gather.20
  381.6 34.7 reduce-scatter.22
  419.7 85.7 reduce-scatter.14
  508.9 84.8 reduce-scatter.12
  596.0 52.8 reduce-scatter.20
  652.4 84.2 reduce-scatter.10
  739.9 84.8 reduce-scatter.8
  827.0 72.8 reduce-scatter.18
  902.2 91.4 reduce-scatter.16
where the time goes:
time: 1030 us
  waiting for transfers between devices  900 us (87%)
  matrix products  64.8 us (6%)
  other arithmetic  27.8 us (3%)
  local copies, waits for them, and re-layouts  18.2 us (2%)
  between operations  14.1 us (1%)
    reduce_scatter x4, waiting for transfers between devices, per_device(): lax.psum_scatter(right_part.reshape(row_step, mesh_rows * BLOCK_SIZE, num...  348 us
    reduce_scatter x4, waiting for transfers between devices, per_device(): lax.psum_scatter(lower_part.reshape(left_rows, col_step, mesh_cols * BLOC...  247 us
    all_gather x4, waiting for transfers between devices, per_device(): lax.all_gather(side_block, 'row', axis=1)  177 us
    all_gather x4, waiting for transfers between devices, per_device(): lax.all_gather(lower_panel.reshape(left_rows, col_step, BLOCK_SIZE), 'col...  127 us
    dot_general x4, matrix products, per_device(): jnp.einsum('rbqe,rf->bqef', gathered, grad_rows, preferred_element_type=j...  32.6 us
    dot_general x4, matrix products, per_device(): jnp.einsum('rf,bqef->rbqe', grad_rows, side_rows, preferred_element_type=...  32.2 us
  transfers between devices with their start and end apart: 16, of which 16 were waited for; matrix products, arithmetic and copies ran while one was open for 8% of the time, Pallas kernels for 0%

commit v1 on v0

v1 whole, which is shorter than its diff:
```python
import heapq

import jax
import jax.numpy as jnp
from jax import lax
from jax.experimental import pallas as pl
from jax.experimental.pallas import tpu as pltpu
from jax.sharding import PartitionSpec as P

BLOCK = 256
MESH = pl.DeviceIdType.MESH
L_RUNS = (((0, 0, 3), (1, 1, 1)), ((1, 2, 3), (2, 2, 3), (3, 3, 3)))


def plan():
    jobs = {}
    for name, first in (("grad", 0), ("side", 1)):
        def hop(off, axis, step):
            moved = list(off)
            moved[axis] = (moved[axis] - step) % 4
            return tuple(moved)
        for half in range(2):
            for lane in [None, 0, 1, 2, 3]:
                axis = first if lane is None else 1 - first
                own = [0, 0]
                if lane is not None:
                    own[first] = lane
                own = tuple(own)
                for step in (1, -1):
                    jobs[(name, own, half, axis, step)] = ((name, own, half), (axis, step), 11.3, (name, hop(own, axis, step), half))
                step = 1 if half == 0 else -1
                near = hop(own, axis, step)
                jobs[(name, near, half, axis, step)] = ((name, near, half), (axis, step), 11.3, (name, hop(near, axis, step), half))
    for name, pieces, cost in (("line", 1, 11.3), ("low", 2, 14.1)):
        for q in range(pieces):
            for half in range(2):
                for step in (1, -1):
                    jobs[(name, (0, 0, q), half, 2, step)] = ((name, (0, 0, q), half), (2, step), cost, (name, (-step % 4, 0, q), half))
                step = 1 if half == 0 else -1
                jobs[(name, (-step % 4, 0, q), half, 2, step)] = ((name, (-step % 4, 0, q), half), (2, step), cost, (name, (2, 0, q), half))
                for off in range(4):
                    jobs[(name, (off, 0, q), half, 3, 1)] = ((name, (off, 0, q), half), (3, 1), cost / 8, (name, (off, 1, q), half))
    ready = {}
    for half in range(2):
        ready[("grad", (0, 0), half)] = 0.0
        ready[("line", (0, 0, 0), half)] = 0.0
        ready[("side", (0, 0), half)] = 30.0
        for q in range(2):
            ready[("low", (0, 0, q), half)] = 50.0 + 10 * q
    waiting = dict(jobs)
    free = {}
    order = []
    while waiting:
        best = None
        for key, (need, link, cost, made) in waiting.items():
            if need in ready:
                start = max(ready[need], free.get(link, 0.0))
                rank = (start, ready[need], str(key))
                if best is None or rank < best[0]:
                    best = (rank, key)
        (start, avail, _), key = best
        need, link, cost, made = waiting.pop(key)
        free[link] = start + cost
        assert made not in ready
        ready[made] = start + cost + 2.5
        order.append((max(avail, start - 12.0), start, key))
    order.sort(key=lambda t: (t[0], t[1]))
    ends = sorted((t, e) for e, t in ready.items())
    return jobs, [key for _, _, key in order], ends


def gather_kernel(low_ref, side_ref, grad_ref, low_all, side_all, grad_all, line_all, stage,
                  low_recv, side_recv, grad_recv, line_recv, send_sem, local_sem):
    r, c = lax.axis_index("row"), lax.axis_index("col")
    z, y, x, core = r // 4, r % 4, c // 2, c % 2

    def place(zz, yy, xx, cc):
        return {"row": zz * 4 + yy, "col": xx * 2 + cc}

    def low_slot(xx, cc, q):
        h = r // 8
        dx = (xx + 4 - (r % 8) // 2) % 4
        dc = (cc + r) % 2
        yy = (dx + h * (4 - 2 * dx)) % 4
        zz = 2 - 2 * h + dc * (4 * h - 2) + q
        return zz * 4 + yy

    def slot(name, off):
        if name in ("grad", "side"):
            return ((z + off[0]) % 4) * 4 + (y + off[1]) % 4
        xx, cc = (x + off[0]) % 4, (core + off[1]) % 2
        if name == "line":
            return xx * 2 + 1 - cc
        return low_slot(xx, cc, off[2])

    bufs = {"grad": (grad_all, grad_recv, 0), "side": (side_all, side_recv, 1),
            "line": (line_all, line_recv, 2), "low": (low_all, low_recv, 3)}

    def local(src, dst, i):
        return pltpu.make_async_copy(src, dst, local_sem.at[i])

    side_row = (r // 8) * 8 + c + 1 - 2 * (c % 2)
    pltpu.make_async_remote_copy(side_ref, side_all.at[side_row], send_sem.at[1], side_recv.at[side_row, 0],
                                 device_id={"row": side_row, "col": r % 8}, device_id_type=MESH).start()

    def send_low():
        for h in range(2):
            xx = (x + (y if h == 0 else 4 - y)) % 4
            same = (z // 2) if h == 1 else 1 - z // 2
            dest = {"row": c + 8 * h, "col": xx * 2 + (core + same) % 2}
            for half in range(2):
                at = 0
                for kb, b0, b1 in L_RUNS[half]:
                    n = (b1 + 1 - b0) * BLOCK
                    pltpu.make_async_remote_copy(
                        low_ref.at[pl.ds(b0 * BLOCK, n), pl.ds((2 * kb + h) * BLOCK, BLOCK)],
                        low_all.at[r, half, pl.ds(at, n)], send_sem.at[3], low_recv.at[r, half],
                        device_id=dest, device_id_type=MESH).start()
                    at += n

    local(grad_ref, stage, 0).start()
    jobs, order, ends = plan()
    waited = set()

    def wait(event):
        if event in waited:
            return
        waited.add(event)
        name, off, half = event
        buf, recv, _ = bufs[name]
        s = slot(name, off)
        if name == "side" and off == (0, 0):
            waited.add((name, off, 1 - half))
            pltpu.make_async_copy(buf.at[s], buf.at[s], recv.at[s, 0]).wait()
            return
        pltpu.make_async_copy(buf.at[s, half], buf.at[s, half], recv.at[s, half]).wait()

    own = {("grad", (0, 0)), ("line", (0, 0, 0))}
    sent_low = False
    for key in order:
        name, off, half, axis, step = key
        buf, recv, i = bufs[name]
        if (name, off) in own:
            src = grad_ref.at[half]
        else:
            if not sent_low:
                send_low()
                sent_low = True
                local(grad_ref, stage, 0).wait()
                local(stage, grad_all.at[slot("grad", (0, 0))], 1).start()
                local(stage, line_all.at[slot("line", (0, 0, 0))], 2).start()
            wait((name, off, half))
            src = buf.at[slot(name, off), half]
        to = [z, y, x, core]
        to[axis] = (to[axis] + step + 4) % 4 if axis < 3 else 1 - core
        s = slot(name, off)
        pltpu.make_async_remote_copy(src, buf.at[s, half], send_sem.at[i], recv.at[s, half],
                                     device_id=place(*to), device_id_type=MESH).start()
    for _, event in ends:
        if event[:2] not in own:
            wait(event)
    local(stage, grad_all.at[slot("grad", (0, 0))], 1).wait()
    local(stage, line_all.at[slot("line", (0, 0, 0))], 2).wait()
    for i, part in ((0, grad_all.at[pl.ds(0, 15)]), (1, side_all), (2, line_all.at[pl.ds(0, 7)]), (3, low_all)):
        pltpu.make_async_copy(part, part, send_sem.at[i]).wait()


def gather(low, side, grad):
    cols = side.shape[1]
    half = (2, 2 * BLOCK, cols)
    piece = (2, 5 * BLOCK, BLOCK)
    dt = low.dtype
    anywhere = pl.BlockSpec(memory_space=pl.ANY)
    return pl.pallas_call(
        gather_kernel,
        out_shape=[jax.ShapeDtypeStruct((16, *piece), dt), jax.ShapeDtypeStruct((16, *half), dt),
                   jax.ShapeDtypeStruct((16, *half), dt), jax.ShapeDtypeStruct((8, *half), dt)],
        in_specs=[anywhere] * 3,
        out_specs=[anywhere] * 4,
        scratch_shapes=[
            pltpu.VMEM(half, dt),
            pltpu.SemaphoreType.DMA((16, 2)),
            pltpu.SemaphoreType.DMA((16, 2)),
            pltpu.SemaphoreType.DMA((16, 2)),
            pltpu.SemaphoreType.DMA((8, 2)),
            pltpu.SemaphoreType.DMA((4,)),
            pltpu.SemaphoreType.DMA((3,)),
        ],
        compiler_params=pltpu.CompilerParams(has_side_effects=True),
        name="gather",
    )(low, side.reshape(half), grad.reshape(half))


def products(low_all, side_all, grad_all, line_all):
    cols = side_all.shape[-1]
    low = low_all.reshape(16, 10, BLOCK, BLOCK)
    grad = grad_all.reshape(16, 4, BLOCK, cols)
    first = (0, 4, 7, 9)
    right = []
    for kb in range(4):
        n = 4 - kb
        right.append(jnp.einsum("rbik,rbij->kj", low[:, first[kb]:first[kb] + n], grad[:, kb:],
                                preferred_element_type=jnp.float32).astype(jnp.bfloat16))
    line = line_all.reshape(8, 4, BLOCK, cols)
    side = side_all.reshape(2, 8, 4, BLOCK, cols)
    lower = []
    for bi in range(4):
        part = jnp.einsum("sif,hskef->ikhe", line[:, bi], side[:, :, :bi + 1], preferred_element_type=jnp.float32)
        part = part.astype(jnp.bfloat16).reshape(BLOCK, (bi + 1) * 2 * BLOCK)
        lower.append(jnp.pad(part, ((0, 0), (0, (3 - bi) * 2 * BLOCK))))
    return jnp.concatenate(right, 0), jnp.concatenate(lower, 0)


def per_device(low, side, grad):
    right, lower = products(*gather(low, side, grad))
    rows_here, cols_here = lower.shape
    row_pos = jnp.arange(rows_here)[:, None]
    col_pos = jnp.arange(cols_here)[None, :]
    row_global = (row_pos // BLOCK * 16 + lax.axis_index("row")) * BLOCK + row_pos % BLOCK
    col_global = (col_pos // BLOCK * 8 + lax.axis_index("col")) * BLOCK + col_pos % BLOCK
    return right, jnp.where(row_global >= col_global, lower, jnp.zeros_like(lower))


def solution(mesh):
    spec = P(("batch", "row"), "col")
    return jax.shard_map(per_device, mesh=mesh, in_specs=(spec,) * 3, out_specs=(spec,) * 2, check_vma=False)
```

time: 1030 us -> 381 us (0.37)
  the two profiles are of different devices: /device:TPU:1 before, /device:TPU:14 now
where the time goes in v1:
time: 381 us
  Pallas kernels  308 us (81%)
  matrix products  58.1 us (15%)
  other arithmetic  6.68 us (2%)
  local copies, waits for them, and re-layouts  6.6 us (2%)
    pallas_call x1, Pallas kernels, gather(): pl.pallas_call(gather_kernel, out_shape=[jax.ShapeDtypeStruct((16, *piece...  308 us
    dot_general x4, matrix products, products(): jnp.einsum('rbik,rbij->kj', low[:, first[kb]:first[kb] + n], grad[:, kb:]...  33.6 us
    dot_general x4, matrix products, products(): jnp.einsum('sif,hskef->ikhe', line[:, bi], side[:, :, :bi + 1], preferred...  24.5 us

profile of v1, /device:TPU:14, one launch (start us, length us, event | category | flops | bytes accessed | tf_op | source)
XLA Modules:
  0.0 380.5 jit_solution(16458812605325931423)
XLA Ops:
  0.6 308.4 %gather.1 = (bf16[16,2,1280,256]{3,2,1,0:T(8,128)(2,1)}, bf16[16,2,512,512]{3,2,1,0:T(8,128)(2,1)}, bf16[16,2,512,512]{3,2,1,0:T(8,128)(2,1)}, bf16[8,2,512,512]{3,2,1,0:T(8,128)(2,1)}) custom-call(bf16[1024,2048]{1,0:T(8,128)(2,1)} %low_ref.1, bf16[2,512,512]{2,1,0:T(8,128)(2,1)} %bitcast.157, bf16[2,512,512]{2,1,0:T(8,128)(2,1)} %bitcast.158), custom_call_target="tpu_custom_call" | custom-call | tf_op jit(solution)/shard_map/gather/pallas_call | solution.py:174
  309.0 4.1 %fusion.50 = bf16[256,512]{1,0:T(8,128)(2,1)S(1)} fusion(bf16[16,10,256,256]{3,2,1,0:T(8,128)(2,1)} %bitcast.160, bf16[16,4,256,512]{3,2,1,0:T(8,128)(2,1)} %bitcast.170), kind=kOutput, calls=%fused_computation.49 | convolution fusion | flops 1073872896 | bytes 6553600 | tf_op jit(solution)/shard_map/rbik,rbij->kj/dot_general | solution.py:202
  313.1 7.0 %fusion.51 = bf16[256,512]{1,0:T(8,128)(2,1)S(1)} fusion(bf16[16,4,256,512]{3,2,1,0:T(8,128)(2,1)} %bitcast.171, bf16[16,10,256,256]{3,2,1,0:T(8,128)(2,1)} %bitcast.161), kind=kOutput, calls=%fused_computation.50 | convolution fusion | flops 2147614720 | bytes 12845056 | tf_op jit(solution)/shard_map/rbik,rbij->kj/dot_general | solution.py:202
  320.1 9.8 %fusion.41 = bf16[256,512]{1,0:T(8,128)(2,1)S(1)} fusion(bf16[16,4,256,512]{3,2,1,0:T(8,128)(2,1)} %bitcast.172, bf16[16,10,256,256]{3,2,1,0:T(8,128)(2,1)} %bitcast.162), kind=kOutput, calls=%fused_computation.46 | convolution fusion | flops 3221356544 | bytes 19136512 | tf_op jit(solution)/shard_map/rbik,rbij->kj/dot_general | solution.py:202
  330.0 12.7 %fusion.46 = bf16[256,512]{1,0:T(8,128)(2,1)S(1)} fusion(bf16[16,4,256,512]{3,2,1,0:T(8,128)(2,1)} %bitcast.173, bf16[16,10,256,256]{3,2,1,0:T(8,128)(2,1)} %bitcast.163), kind=kOutput, calls=%fused_computation.47 | convolution fusion | flops 4295098368 | bytes 25427968 | tf_op jit(solution)/shard_map/rbik,rbij->kj/dot_general | solution.py:202
  342.6 1.0 pad_maximum_fusion
  343.7 0.0 slice-start
  343.7 0.0 slice-start.1
  343.7 0.0 slice-start.2
  343.7 8.8 %fusion.24 = bf16[256,3,2,256]{0,3,1,2:T(8,128)(2,1)S(1)} fusion(bf16[2,8,4,256,512]{4,3,2,1,0:T(8,128)(2,1)} %bitcast.164, bf16[8,4,256,512]{3,2,1,0:T(8,128)(2,1)} %bitcast.174), kind=kOutput, calls=%fused_computation.39 | convolution fusion | flops 3221618688 | bytes 19660800 | tf_op jit(solution)/shard_map/sif,hskef->ikhe/dot_general | solution.py:208
  352.5 0.1 copy.37
  352.5 0.0 slice-start.3
  352.5 6.7 %fusion.35 = bf16[256,2,2,256]{0,3,1,2:T(8,128)(2,1)S(1)} fusion(bf16[2,8,4,256,512]{4,3,2,1,0:T(8,128)(2,1)} %bitcast.165, bf16[8,4,256,512]{3,2,1,0:T(8,128)(2,1)} %bitcast.175), kind=kOutput, calls=%fused_computation.44 | convolution fusion | flops 2147745792 | bytes 19398656 | tf_op jit(solution)/shard_map/sif,hskef->ikhe/dot_general | solution.py:208
  359.3 0.0 slice-done
  359.3 0.0 slice-done.1
  359.3 0.0 slice-done.2
  359.3 0.0 slice-done.3
  359.3 2.9 fusion.49
  362.2 6.2 %fusion.21 = bf16[256,4,2,256]{0,3,1,2:T(8,128)(2,1)S(1)} fusion(bf16[2,8,4,256,512]{4,3,2,1,0:T(8,128)(2,1)S(1)} %bitcast.169, bf16[8,4,256,512]{3,2,1,0:T(8,128)(2,1)} %bitcast.177), kind=kOutput, calls=%fused_computation.36 | convolution fusion | flops 4295491584 | bytes 19922944 | tf_op jit(solution)/shard_map/sif,hskef->ikhe/dot_general | solution.py:208
  368.4 0.1 copy.40
  368.5 5.6 %compare_select_fusion = bf16[1024,2048]{0,1:T(8,128)(2,1)} fusion(bf16[256,1536]{0,1:T(8,128)(2,1)S(1)} %bitcast.155, bf16[256,1024]{0,1:T(8,128)(2,1)S(1)} %bitcast.156, bf16[256,512]{0,1:T(8,128)(2,1)S(1)} %bitcast.159, bf16[256,2048]{0,1:T(8,128)(2,1)S(1)} %bitcast.154, s32[1024]{0:T(1024)S(1)} %fusion.76, s32[2048]{0:T(1024)S(1)} %fusion.65), kind=kLoop, calls=%fused_computation.16 | loop fusion | flops 41943040 | bytes 6828032 | tf_op jit(solution)/shard_map/jit(_where)/select_n | solution.py:221
  374.1 6.4 %copy.41 = bf16[1024,2048]{1,0:T(8,128)(2,1)} copy(bf16[1024,2048]{0,1:T(8,128)(2,1)} %compare_select_fusion) | data formatting | bytes 8388608
  (4 shorter events, 0.1 us)
Async XLA Ops:
  343.7 15.6 %slice-start = ((s8[16777216]{0:T(1024)(128)(4,1)}), s8[4194304]{0:T(1024)(128)(4,1)S(1)}, s32[]{:S(2)}) async-start(s8[16777216]{0:T(1024)(128)(4,1)} %bitcast.166), calls=%async_computation | async-start | bytes 8388608
  343.7 15.6 %slice-start.1 = ((s8[16777216]{0:T(1024)(128)(4,1)}), s8[4194304]{0:T(1024)(128)(4,1)S(1)}, s32[]{:S(2)}) async-start(s8[16777216]{0:T(1024)(128)(4,1)} %bitcast.166), calls=%async_computation.1 | async-start | bytes 8388608
  343.7 15.6 %slice-start.2 = ((s8[16777216]{0:T(1024)(128)(4,1)}), s8[4194304]{0:T(1024)(128)(4,1)S(1)}, s32[]{:S(2)}) async-start(s8[16777216]{0:T(1024)(128)(4,1)} %bitcast.166), calls=%async_computation.2 | async-start | bytes 8388608
  352.5 6.8 %slice-start.3 = ((s8[16777216]{0:T(1024)(128)(4,1)}), s8[4194304]{0:T(1024)(128)(4,1)S(1)}, s32[]{:S(2)}) async-start(s8[16777216]{0:T(1024)(128)(4,1)} %bitcast.166), calls=%async_computation.3 | async-start | bytes 8388608

commit v2 on v0

v2 whole, which is shorter than its diff:
```python
import jax
import jax.numpy as jnp
from jax import lax
from jax.experimental import pallas as pl
from jax.experimental.pallas import tpu as pltpu
from jax.sharding import PartitionSpec as P

BLOCK = 256
MESH = pl.DeviceIdType.MESH
NROWS = (1024, 768, 512, 256)
FIRST = (0, 1024, 1792, 2304)
LAG = 2.5


def plan():
    ready, jobs, steps = {}, [], []

    def job(need, link, cost, made, prio, step):
        jobs.append((need, link, cost, made, prio, step))

    for q in range(4):
        first = 1 if q < 2 else 0
        def hop(off, axis, d):
            moved = list(off)
            moved[axis] = (moved[axis] - d) % 4
            return tuple(moved)
        ready[("side", (0, 0), q)] = 24.0
        for lane in (None, 0, 1, 3, 2):
            axis = first if lane is None else 1 - first
            own = [0, 0]
            if lane is not None:
                own[first] = lane
            own = tuple(own)
            prio = 1 if lane is None else 5
            for d in (1, -1):
                job(("side", own, q), ("zy"[axis], d), 5.65, ("side", hop(own, axis, d), q), prio, ("side", own, q, axis, d))
            d = 1 if q % 2 == 0 else -1
            near = hop(own, axis, d)
            job(("side", near, q), ("zy"[axis], d), 5.65, ("side", hop(near, axis, d), q), prio, ("side", near, q, axis, d))
    for half in range(2):
        ready[("grad", 0, half)] = 0.0
        ready[("line", "own", half)] = 0.0
        for d in (1, -1):
            job(("grad", 0, half), ("z", d), 11.3, ("grad", -d % 4, half), 3, ("grad", 0, half, d))
        d = 1 if half == 0 else -1
        job(("grad", -d % 4, half), ("z", d), 11.3, ("grad", 2, half), 3, ("grad", -d % 4, half, d))
        for to in "ab":
            job(("line", "own", half), to, 11.3, ("line", to, half), 4, ("line", "own", half, to))
        src, to = ("a", "b") if half == 0 else ("b", "a")
        job(("line", src, half), to, 11.3, ("line", "o", half), 4, ("line", src, half, to))
        for piece in ("own", "a", "b", "o"):
            job(("line", piece, half), "sib", 1.0, ("line", piece + "s", half), 4, ("line", piece, half, "sib"))
    done = 2.0
    for kb in range(4):
        cost = 11.3 * NROWS[kb] / 1024
        done += 1.5 * cost
        for zz in range(4):
            ready[("hub", kb, zz)] = done
            job(("hub", kb, zz), "b", cost, ("p", kb, zz), 2, ("hub", kb, zz))
            job(("p", kb, zz), "a", cost, ("q", kb, zz), 2, ("p", kb, zz))
            job(("q", kb, zz), "sib", 0.1 * cost, ("qs", kb, zz), 2, ("q", kb, zz))
    free = {("z", 1): 20.0, ("z", -1): 20.0}
    pending = list(jobs)
    while pending:
        best = min((j for j in pending if j[0] in ready),
                   key=lambda j: (max(ready[j[0]], free.get(j[1], 0.0)), j[4], ready[j[0]]))
        pending.remove(best)
        need, link, cost, made, prio, step = best
        start = max(ready[need], free.get(link, 0.0))
        free[link] = start + cost
        ready[made] = start + cost + LAG
        steps.append((max(ready[need], start - 12.0), start, ("send",) + step))
        for kb in range(4):
            key = ("sum", kb)
            if key not in ready and all(("qs", kb, zz) in ready for zz in range(4)):
                now = max(ready[("qs", kb, zz)] for zz in range(4)) + 3.0
                ready[key] = now
                steps.append((now, now, ("part", kb)))
                for d in (1, -1):
                    pending.append((key, ("y", d), 5.65, ("hop", kb, d), 0, ("far", kb, d)))
                    pending.append((("hop", kb, d), ("y", d), 11.3, ("got", kb, d), 0, ("near", kb, d)))
    slots = sorted((max(ready[("side", (a, b), q)] for q in range(4)), (a, b)) for a in range(4) for b in range(4))
    for g in range(4):
        now = max(max(t for t, _ in slots[4 * g:4 * g + 4]), max(t for e, t in ready.items() if e[0] == "line")) + 1.0
        steps.append((now, now, ("dot", tuple(off for _, off in slots[4 * g:4 * g + 4]))))
    steps.sort(key=lambda t: (t[0], t[1]))
    return [s for _, _, s in steps], ready


def kernel(low_ref, side_ref, grad_ref, right_ref, lower_ref, low_all,
           side_all, grad_all, line_all, acc, part, hop, got, lbuf, stage, obuf, rbuf,
           low_recv, side_recv, grad_recv, line_recv, hop_recv, got_recv, send_sem, lbuf_sem, stage_sem, out_sem):
    r, c = lax.axis_index("row"), lax.axis_index("col")
    z, y, x, core = r // 4, r % 4, c // 2, c % 2
    hub = x // 2 == z % 2
    xa, xb = x + 1 - 2 * (x % 2), 3 - x
    xh = jnp.where(hub, x, xb)

    def bxor(a, b):
        return sum(((a // n % 2 + b // n % 2) % 2) * n for n in (1, 2, 4))

    def place(zz, yy, xx, cc):
        return {"row": zz * 4 + yy, "col": xx * 2 + cc}

    def remote(src, dst, send, recv, to):
        return pltpu.make_async_remote_copy(src, dst, send_sem.at[send], recv, device_id=to, device_id_type=MESH)

    def arrive(ref, sem):
        pltpu.make_async_copy(ref, ref, sem).wait()

    sib = place(z, y, x, 1 - core)
    up, down = place(z, (y + 1) % 4, x, core), place(z, (y + 3) % 4, x, core)

    side_row = (r // 8) * 8 + bxor(c, r % 8)
    side_self = (side_row == r) & (c == r % 8)
    for q in range(4):
        @pl.when(jnp.logical_not(side_self))
        def _():
            remote(side_ref.at[q], side_all.at[side_row, pl.ds(q * BLOCK, BLOCK)], 0, side_recv.at[side_row, q],
                   {"row": side_row, "col": r % 8}).start()

        @pl.when(side_self)
        def _():
            pltpu.make_async_copy(side_ref.at[q], side_all.at[side_row, pl.ds(q * BLOCK, BLOCK)], side_recv.at[side_row, q]).start()

    mine = 2 * (x % 2) + core

    def low_piece(h, kb):
        return low_ref.at[pl.ds(kb * BLOCK, NROWS[kb]), pl.ds(pl.multiple_of((2 * kb + h) * BLOCK, BLOCK), BLOCK)]

    def low_at(yy, zz, kb):
        return low_all.at[yy, zz, pl.ds(FIRST[kb], NROWS[kb])]

    def stage_at(kb):
        return stage.at[pl.ds(FIRST[kb], NROWS[kb])]

    here = z // 2

    @pl.when(hub)
    def _():
        for kb in range(4):
            pltpu.make_async_copy(low_piece(here, kb), stage_at(kb), stage_sem.at[kb]).start()
            remote(low_piece(1 - here, kb), low_at(mine, z, kb), 1, low_recv.at[mine, z, kb],
                   place((z + 2) % 4, y, x, core)).start()

    @pl.when(jnp.logical_not(hub))
    def _():
        for kb in range(4):
            for h in range(2):
                remote(low_piece(h, kb), low_at(mine, z, kb), 1, low_recv.at[mine, z, kb],
                       place(x // 2 + 2 * h, y, x, core)).start()

    own_grad = pltpu.make_async_copy(grad_ref, grad_all.at[z], out_sem.at[0])
    own_line = pltpu.make_async_copy(grad_ref, line_all.at[c], out_sem.at[1])
    own_grad.start()
    own_line.start()

    @pl.when(hub)
    def _():
        for kb in range(4):
            pltpu.make_async_copy(low_piece(here, kb), stage_at(kb), stage_sem.at[kb]).wait()
            pltpu.make_async_copy(stage_at(kb), low_at(mine, z, kb), low_recv.at[mine, z, kb]).start()

    steps, ready = plan()
    waited = set()

    def line_slot(piece):
        xx = {"own": x, "a": xa, "b": xb, "o": (x + 2) % 4}[piece.rstrip("s")]
        return xx * 2 + (1 - core if piece.endswith("s") else core)

    def half_at(ref, slot, half):
        return ref.at[slot, pl.ds(half * 512, 512)]

    def wait(event):
        if event in waited:
            return
        waited.add(event)
        name = event[0]
        if name == "side":
            slot = ((z + event[1][0]) % 4) * 4 + (y + event[1][1]) % 4
            arrive(side_all.at[slot, pl.ds(event[2] * BLOCK, BLOCK)], side_recv.at[slot, event[2]])
        elif name == "grad":
            slot = (z + event[1]) % 4
            arrive(half_at(grad_all, slot, event[2]), grad_recv.at[slot, event[2]])
        elif name == "line":
            slot = line_slot(event[1])
            arrive(half_at(line_all, slot, event[2]), line_recv.at[slot, event[2]])
        else:
            yy = 2 * (xh % 2 if name in ("p", "ps") else 1 - xh % 2) + (1 - core if name.endswith("s") else core)
            arrive(low_at(yy, event[2], event[1]), low_recv.at[yy, event[2], event[1]])

    def low_send(yy, zz, kb, send, to):
        remote(low_at(yy, zz, kb), low_at(yy, zz, kb), send, low_recv.at[yy, zz, kb], to).start()

    def send(step):
        name = step[0]
        if name == "side":
            _, off, q, axis, d = step
            wait(("side", off, q))
            slot = ((z + off[0]) % 4) * 4 + (y + off[1]) % 4
            to = place((z + d + 4) % 4, y, x, core) if axis == 0 else place(z, (y + d + 4) % 4, x, core)
            ref = side_all.at[slot, pl.ds(q * BLOCK, BLOCK)]
            remote(ref, ref, 2, side_recv.at[slot, q], to).start()
        elif name == "grad":
            _, off, half, d = step
            if off:
                wait(("grad", off, half))
            slot = (z + off) % 4
            src = half_at(grad_all, slot, half) if off else grad_ref.at[pl.ds(half * 512, 512)]
            remote(src, half_at(grad_all, slot, half), 3, grad_recv.at[slot, half], place((z + d + 4) % 4, y, x, core)).start()
        elif name == "line":
            _, piece, half, to = step
            if piece != "own":
                wait(("line", piece, half))
            slot = line_slot(piece)
            src = half_at(line_all, slot, half) if piece != "own" else grad_ref.at[pl.ds(half * 512, 512)]
            dest = {"a": place(z, y, xa, core), "b": place(z, y, xb, core), "sib": sib}[to]
            remote(src, half_at(line_all, slot, half), 4, line_recv.at[slot, half], dest).start()
        elif name == "hub":
            _, kb, zz = step

            @pl.when(hub)
            def _():
                yy = mine
                arrive(low_at(yy, zz, kb), low_recv.at[yy, zz, kb])
                low_send(yy, zz, kb, 5, place(z, y, xb, core))
                low_send(yy, zz, kb, 5, place(z, y, xa, core))
                low_send(yy, zz, kb, 6, sib)
        elif name == "p":
            _, kb, zz = step
            yy = 2 * (xb % 2) + core

            @pl.when(jnp.logical_not(hub))
            def _():
                arrive(low_at(yy, zz, kb), low_recv.at[yy, zz, kb])
                low_send(yy, zz, kb, 5, place(z, y, xa, core))
                low_send(yy, zz, kb, 6, sib)
        elif name == "q":
            _, kb, zz = step
            wait(("q", kb, zz))
            low_send(2 * (1 - xh % 2) + core, zz, kb, 6, sib)
        elif name == "far":
            _, kb, d = step
            i = 0 if d == 1 else 1
            rows = pl.ds(i * 128, 128)
            remote(part.at[kb, 0, rows], hop.at[kb, i], 7, hop_recv.at[kb, i], up if d == 1 else down).start()
        elif name == "near":
            _, kb, d = step
            i, t = (0, 3) if d == 1 else (1, 1)
            arrive(hop.at[kb, i], hop_recv.at[kb, i])
            rows = pl.ds(i * 128, 128)
            part[kb, t, rows] += hop[kb, i]
            remote(part.at[kb, t], got.at[kb, i], 8, got_recv.at[kb, i], up if d == 1 else down).start()

    def add_part(kb):
        for zz in range(4):
            for name in ("ps", "q", "qs"):
                wait((name, kb, zz))
        if kb == 0:
            own_grad.wait()
            for off in (1, 2, 3):
                for half in range(2):
                    wait(("grad", off, half))
        n = NROWS[kb]

        def load(t):
            return pltpu.make_async_copy(low_all.at[(y + 2 + t) % 4, :, pl.ds(FIRST[kb], n)],
                                         lbuf.at[t % 2, :, pl.ds(0, n)], lbuf_sem.at[t % 2])

        load(0).start()

        def body(t, carry):
            @pl.when(t < 3)
            def _():
                load(t + 1).start()
            load(t).wait()
            total = jnp.zeros((BLOCK, 512), jnp.float32)
            for zz in range(4):
                total += lax.dot_general(lbuf[t % 2, zz, pl.ds(0, n)], grad_all[zz, pl.ds(kb * BLOCK, n)],
                                         (((0,), (0,)), ((), ())), preferred_element_type=jnp.float32)
            part[kb, t] = total
            return carry

        lax.fori_loop(0, 4, body, 0)

    def add_dot(offs, start):
        if start:
            own_line.wait()
            for piece in ("a", "b", "o", "owns", "as", "bs", "os"):
                for half in range(2):
                    wait(("line", piece, half))
            acc[...] = jnp.zeros_like(acc)
        slots = []
        for off in offs:
            for q in range(4):
                wait(("side", off, q))
            slots.append(((z + off[0]) % 4) * 4 + (y + off[1]) % 4)

        def body(i, carry):
            slot = slots[3]
            for n in range(3):
                slot = jnp.where(i == n, slots[n], slot)
            h, cj = slot // 8, bxor(slot % 8, c)
            for bi in range(4):
                n = (bi + 1) * BLOCK
                acc[h, bi, :, :n] += lax.dot_general(
                    line_all[cj, bi * BLOCK:(bi + 1) * BLOCK], side_all[slot, :n],
                    (((1,), (1,)), ((), ())), preferred_element_type=jnp.float32)
            return carry

        lax.fori_loop(0, 4, body, 0)

    started = False
    for step in steps:
        if step[0] == "send":
            send(step[1:])
        elif step[0] == "part":
            add_part(step[1])
        else:
            add_dot(step[1], not started)
            started = True

    for bi in range(4):
        if bi >= 2:
            pltpu.make_async_copy(obuf.at[bi % 2], lower_ref.at[pl.ds((bi - 2) * BLOCK, BLOCK)], out_sem.at[2 + bi % 2]).wait()
        for kb in range(4):
            for h in range(2):
                cols = pl.ds((2 * kb + h) * BLOCK, BLOCK)
                if kb <= bi:
                    obuf[bi % 2, :, cols] = acc[h, bi, :, kb * BLOCK:(kb + 1) * BLOCK].astype(jnp.bfloat16)
                else:
                    obuf[bi % 2, :, cols] = jnp.zeros((BLOCK, BLOCK), jnp.bfloat16)
        pltpu.make_async_copy(obuf.at[bi % 2], lower_ref.at[pl.ds(bi * BLOCK, BLOCK)], out_sem.at[2 + bi % 2]).start()
    for kb in range(4):
        for i in range(2):
            arrive(got.at[kb, i], got_recv.at[kb, i])
        rbuf[kb * BLOCK:(kb + 1) * BLOCK] = (part[kb, 2] + got[kb, 0] + got[kb, 1]).astype(jnp.bfloat16)
    out = pltpu.make_async_copy(rbuf, right_ref, out_sem.at[4])
    out.start()

    def sent(ref, i):
        pltpu.make_async_copy(ref, ref, send_sem.at[i]).wait()

    def pieces(n):
        return low_all.at[pl.ds(0, n // 4)] if n >= 4 else low_all.at[0, pl.ds(0, n)]

    @pl.when(jnp.logical_not(side_self))
    def _():
        sent(side_all.at[0], 0)

    @pl.when(hub)
    def _():
        sent(pieces(1), 1)
        sent(pieces(8), 5)

    @pl.when(jnp.logical_not(hub))
    def _():
        sent(pieces(2), 1)
        sent(pieces(4), 5)

    sent(side_all.at[pl.ds(0, 15)], 2)
    sent(grad_all.at[pl.ds(0, 3)], 3)
    sent(line_all.at[pl.ds(0, 7)], 4)
    sent(pieces(8), 6)
    sent(part.at[:, 0], 7)
    sent(got, 8)
    for bi in (2, 3):
        pltpu.make_async_copy(obuf.at[bi % 2], lower_ref.at[pl.ds(bi * BLOCK, BLOCK)], out_sem.at[2 + bi % 2]).wait()
    out.wait()


def fused(low, side, grad):
    dt = low.dtype
    f32 = jnp.float32
    anywhere = pl.BlockSpec(memory_space=pl.ANY)
    dma = pltpu.SemaphoreType.DMA
    return pl.pallas_call(
        kernel,
        out_shape=[jax.ShapeDtypeStruct(grad.shape, dt), jax.ShapeDtypeStruct(low.shape, dt),
                   jax.ShapeDtypeStruct((4, 4, 2560, BLOCK), dt)],
        in_specs=[anywhere] * 3,
        out_specs=[anywhere] * 3,
        scratch_shapes=[
            pltpu.VMEM((16, 1024, 512), dt),
            pltpu.VMEM((4, 1024, 512), dt),
            pltpu.VMEM((8, 1024, 512), dt),
            pltpu.VMEM((2, 4, BLOCK, 1024), f32),
            pltpu.VMEM((4, 4, BLOCK, 512), f32),
            pltpu.VMEM((4, 2, 128, 512), f32),
            pltpu.VMEM((4, 2, BLOCK, 512), f32),
            pltpu.VMEM((2, 4, 1024, BLOCK), dt),
            pltpu.VMEM((2560, BLOCK), dt),
            pltpu.VMEM((2, BLOCK, 2048), dt),
            pltpu.VMEM((1024, 512), dt),
            dma((4, 4, 4)), dma((16, 4)), dma((4, 2)), dma((8, 2)), dma((4, 2)), dma((4, 2)),
            dma((9,)), dma((2,)), dma((4,)), dma((5,)),
        ],
        compiler_params=pltpu.CompilerParams(has_side_effects=True, vmem_limit_bytes=67043328),
        name="fused",
    )(low, side.reshape(4, BLOCK, 512), grad)


def per_device(low, side, grad):
    right, lower, _ = fused(low, side, grad)
    row_pos = jnp.arange(lower.shape[0])[:, None]
    col_pos = jnp.arange(lower.shape[1])[None, :]
    row_global = (row_pos // BLOCK * 16 + lax.axis_index("row")) * BLOCK + row_pos % BLOCK
    col_global = (col_pos // BLOCK * 8 + lax.axis_index("col")) * BLOCK + col_pos % BLOCK
    return right, jnp.where(row_global >= col_global, lower, jnp.zeros_like(lower))


def solution(mesh):
    spec = P(("batch", "row"), "col")
    return jax.shard_map(per_device, mesh=mesh, in_specs=(spec,) * 3, out_specs=(spec,) * 2, check_vma=False)
```

time: 1030 us -> 254 us (0.25)
  waiting for transfers between devices: 900 us -> 0 us
  Pallas kernels: 0 us -> 246 us
  matrix products: 64.8 us -> 0 us
  other arithmetic: 27.8 us -> 4.34 us
  local copies, waits for them, and re-layouts: 18.2 us -> 0.97 us
  between operations: 14.1 us -> 0.67 us
    reduce_scatter x8 -> x0, waiting for transfers between devices: 594 us -> none  [the longest x4 348 us: per_device(): lax.psum_scatter(right_part.reshape(row_step, mesh_rows * BLOCK_SIZE, num...]
    all_gather x8 -> x0, waiting for transfers between devices: 304 us -> none  [the longest x4 177 us: per_device(): lax.all_gather(side_block, 'row', axis=1)]
    pallas_call x0 -> x1, Pallas kernels: none -> 246 us  [fused(): pl.pallas_call(kernel, out_shape=[jax.ShapeDtypeStruct(grad.shape, dt), j...]
    dot_general x8 -> x0, matrix products: 64.8 us -> none  [the longest x4 32.6 us: per_device(): jnp.einsum('rbqe,rf->bqef', gathered, grad_rows, preferred_element_type=j...]
    select_n x1, other arithmetic: 16.9 us -> 4.33 us  [per_device(): jnp.where(row_global >= col_global, lower, jnp.zeros_like(lower))]
  transfers between devices with their start and end apart: 16 -> 0, of which waited for: 16 -> 0; matrix products, arithmetic and copies ran while one was open for 8% -> 0% of each run, Pallas kernels for 0% -> 0%
where the time goes in v2:
time: 254 us; the launch traced here: 252 us
  Pallas kernels  246 us (97%)
  other arithmetic  4.34 us (2%)
    pallas_call x1, Pallas kernels, fused(): pl.pallas_call(kernel, out_shape=[jax.ShapeDtypeStruct(grad.shape, dt), j...  246 us

profile of v2, /device:TPU:1, one launch (start us, length us, event | category | flops | bytes accessed | tf_op | source)
XLA Modules:
  0.0 252.2 jit_solution(10423150669471223057)
XLA Ops:
  0.6 246.2 %fused.1 = (bf16[1024,512]{1,0:T(8,128)(2,1)}, bf16[1024,2048]{1,0:T(8,128)(2,1)}, bf16[4,4,2560,256]{3,2,1,0:T(8,128)(2,1)}) custom-call(bf16[1024,2048]{1,0:T(8,128)(2,1)} %low_ref.1, bf16[4,256,512]{2,1,0:T(8,128)(2,1)} %bitcast.1, bf16[1024,512]{1,0:T(8,128)(2,1)} %grad_ref.1), custom_call_target="tpu_custom_call" | custom-call | tf_op jit(solution)/shard_map/fused/pallas_call | solution.py:377
  246.9 0.0 copy-start
  246.9 4.3 %compare_select_fusion = bf16[1024,2048]{1,0:T(8,128)(2,1)} fusion(bf16[1024,2048]{1,0:T(8,128)(2,1)} %get-tuple-element.5, s32[2048]{0:T(1024)S(1)} %fusion.9, s32[1024]{0:T(1024)S(1)} %fusion.20), kind=kLoop, calls=%fused_computation | loop fusion | flops 4194304 | bytes 8400896 | tf_op jit(solution)/shard_map/jit(_where)/select_n | solution.py:409
  251.2 0.0 copy-done
  251.2 1.0 copy.6
  (2 shorter events, 0.0 us)
Async XLA Ops:
  246.9 4.3 %copy-start = (bf16[1024,512]{1,0:T(8,128)(2,1)S(1)}, bf16[1024,512]{1,0:T(8,128)(2,1)}, u32[]{:S(2)}) copy-start(bf16[1024,512]{1,0:T(8,128)(2,1)} %get-tuple-element.8) | copy-start | bytes 3145732

commit v3 on v2

--- a/solution.py
+++ b/solution.py
@@ -24,7 +24,8 @@
             moved = list(off)
             moved[axis] = (moved[axis] - d) % 4
             return tuple(moved)
-        ready[("side", (0, 0), q)] = 24.0
+        ready[("mid", q)] = 8.0 + 6.0 * q
+        job(("mid", q), "spread", 6.0, ("side", (0, 0), q), 0, ("spread", q))
         for lane in (None, 0, 1, 3, 2):
             axis = first if lane is None else 1 - first
             own = [0, 0]
@@ -50,16 +51,17 @@
         job(("line", src, half), to, 11.3, ("line", "o", half), 4, ("line", src, half, to))
         for piece in ("own", "a", "b", "o"):
             job(("line", piece, half), "sib", 1.0, ("line", piece + "s", half), 4, ("line", piece, half, "sib"))
-    done = 2.0
+    ready[("move", 0)] = 0.0
     for kb in range(4):
         cost = 11.3 * NROWS[kb] / 1024
-        done += 1.5 * cost
+        for d in (1, -1):
+            job(("move", kb), ("z", d), 1.5 * cost, ("move", kb + 1) if d == 1 else ("moved", kb), (0, 0, 4, 4)[kb], ("move", kb, d))
         for zz in range(4):
-            ready[("hub", kb, zz)] = done
-            job(("hub", kb, zz), "b", cost, ("p", kb, zz), 2, ("hub", kb, zz))
-            job(("p", kb, zz), "a", cost, ("q", kb, zz), 2, ("p", kb, zz))
+            job(("hub", kb, zz), "b", cost, ("p", kb, zz), 2 + 0.1 * kb, ("hub", kb, zz))
+            job(("p", kb, zz), "a", cost, ("q", kb, zz), 2 + 0.1 * kb, ("p", kb, zz))
             job(("q", kb, zz), "sib", 0.1 * cost, ("qs", kb, zz), 2, ("q", kb, zz))
-    free = {("z", 1): 20.0, ("z", -1): 20.0}
+        ready[("hub", kb, 0)] = 4.0 + kb
+    free = {}
     pending = list(jobs)
     while pending:
         best = min((j for j in pending if j[0] in ready),
@@ -69,11 +71,15 @@
         start = max(ready[need], free.get(link, 0.0))
         free[link] = start + cost
         ready[made] = start + cost + LAG
+        if made[0] == "move":
+            ready[made] = start + cost
+            for zz, extra in ((1, 0.0), (3, 0.0), (2, cost / 3)):
+                ready[("hub", step[1], zz)] = start + cost + LAG + extra
         steps.append((max(ready[need], start - 12.0), start, ("send",) + step))
         for kb in range(4):
             key = ("sum", kb)
-            if key not in ready and all(("qs", kb, zz) in ready for zz in range(4)):
-                now = max(ready[("qs", kb, zz)] for zz in range(4)) + 3.0
+            if key not in ready and all(("qs", kb, zz) in ready for zz in range(4)) and ("grad", 2, 0) in ready and ("grad", 2, 1) in ready:
+                now = max(t for e, t in ready.items() if e[:2] == ("qs", kb) or e[0] == "grad") + 3.0
                 ready[key] = now
                 steps.append((now, now, ("part", kb)))
                 for d in (1, -1):
@@ -81,15 +87,15 @@
                     pending.append((("hop", kb, d), ("y", d), 11.3, ("got", kb, d), 0, ("near", kb, d)))
     slots = sorted((max(ready[("side", (a, b), q)] for q in range(4)), (a, b)) for a in range(4) for b in range(4))
     for g in range(4):
-        now = max(max(t for t, _ in slots[4 * g:4 * g + 4]), max(t for e, t in ready.items() if e[0] == "line")) + 1.0
-        steps.append((now, now, ("dot", tuple(off for _, off in slots[4 * g:4 * g + 4]))))
+        steps.append((1e4 + (g // 2) * 10, g, ("dot", tuple(off for _, off in slots[4 * g:4 * g + 4]))))
+    steps = [(1e4 + 5, b, s) if s[:3] == ("send", "near", 3) else (a, b, s) for a, b, s in steps]
     steps.sort(key=lambda t: (t[0], t[1]))
     return [s for _, _, s in steps], ready
 
 
 def kernel(low_ref, side_ref, grad_ref, right_ref, lower_ref, low_all,
            side_all, grad_all, line_all, acc, part, hop, got, lbuf, stage, obuf, rbuf,
-           low_recv, side_recv, grad_recv, line_recv, hop_recv, got_recv, send_sem, lbuf_sem, stage_sem, out_sem):
+           mid, low_recv, side_recv, grad_recv, line_recv, hop_recv, got_recv, mid_recv, send_sem, lbuf_sem, stage_sem, out_sem):
     r, c = lax.axis_index("row"), lax.axis_index("col")
     z, y, x, core = r // 4, r % 4, c // 2, c % 2
     hub = x // 2 == z % 2
@@ -111,17 +117,39 @@
     sib = place(z, y, x, 1 - core)
     up, down = place(z, (y + 1) % 4, x, core), place(z, (y + 3) % 4, x, core)
 
-    side_row = (r // 8) * 8 + bxor(c, r % 8)
-    side_self = (side_row == r) & (c == r % 8)
-    for q in range(4):
-        @pl.when(jnp.logical_not(side_self))
+    turn = bxor(c, r % 8)
+    side_row = (r // 8) * 8 + turn
+
+    def quarter(ref, q):
+        return ref.at[pl.ds(q * BLOCK, BLOCK)]
+
+    @pl.when((c != 0) & (turn != 0))
+    def _():
+        for q in range(4):
+            remote(quarter(side_ref, q), quarter(mid, q), 0, mid_recv.at[q], {"row": side_row, "col": c}).start()
+
+    @pl.when((c != 0) & (turn == 0))
+    def _():
+        for q in range(4):
+            remote(quarter(side_ref, q), quarter(side_all.at[side_row], q), 0, side_recv.at[side_row, q],
+                   {"row": side_row, "col": c}).start()
+
+    @pl.when((c == 0) & (turn == 0))
+    def _():
+        for q in range(4):
+            pltpu.make_async_copy(quarter(side_ref, q), quarter(side_all.at[r], q), side_recv.at[r, q]).start()
+
+    def spread(q):
+        to = {"row": r, "col": turn}
+
+        @pl.when((r % 8 != 0) & (c != 0))
         def _():
-            remote(side_ref.at[q], side_all.at[side_row, pl.ds(q * BLOCK, BLOCK)], 0, side_recv.at[side_row, q],
-                   {"row": side_row, "col": r % 8}).start()
-
-        @pl.when(side_self)
+            arrive(quarter(mid, q), mid_recv.at[q])
+            remote(quarter(mid, q), quarter(side_all.at[r], q), 9, side_recv.at[r, q], to).start()
+
+        @pl.when((r % 8 != 0) & (c == 0))
         def _():
-            pltpu.make_async_copy(side_ref.at[q], side_all.at[side_row, pl.ds(q * BLOCK, BLOCK)], side_recv.at[side_row, q]).start()
+            remote(quarter(side_ref, q), quarter(side_all.at[r], q), 9, side_recv.at[r, q], to).start()
 
     mine = 2 * (x % 2) + core
 
@@ -140,15 +168,20 @@
     def _():
         for kb in range(4):
             pltpu.make_async_copy(low_piece(here, kb), stage_at(kb), stage_sem.at[kb]).start()
+
+    def move(kb):
+        @pl.when(hub)
+        def _():
             remote(low_piece(1 - here, kb), low_at(mine, z, kb), 1, low_recv.at[mine, z, kb],
                    place((z + 2) % 4, y, x, core)).start()
 
-    @pl.when(jnp.logical_not(hub))
-    def _():
-        for kb in range(4):
+        @pl.when(jnp.logical_not(hub))
+        def _():
             for h in range(2):
                 remote(low_piece(h, kb), low_at(mine, z, kb), 1, low_recv.at[mine, z, kb],
                        place(x // 2 + 2 * h, y, x, core)).start()
+
+    move(0)
 
     own_grad = pltpu.make_async_copy(grad_ref, grad_all.at[z], out_sem.at[0])
     own_line = pltpu.make_async_copy(grad_ref, line_all.at[c], out_sem.at[1])
@@ -187,14 +220,20 @@
             arrive(half_at(line_all, slot, event[2]), line_recv.at[slot, event[2]])
         else:
             yy = 2 * (xh % 2 if name in ("p", "ps") else 1 - xh % 2) + (1 - core if name.endswith("s") else core)
-            arrive(low_at(yy, event[2], event[1]), low_recv.at[yy, event[2], event[1]])
+            zz = (z + event[2]) % 4
+            arrive(low_at(yy, zz, event[1]), low_recv.at[yy, zz, event[1]])
 
     def low_send(yy, zz, kb, send, to):
         remote(low_at(yy, zz, kb), low_at(yy, zz, kb), send, low_recv.at[yy, zz, kb], to).start()
 
     def send(step):
         name = step[0]
-        if name == "side":
+        if name == "spread":
+            spread(step[1])
+        elif name == "move":
+            if step[1] and step[2] == 1:
+                move(step[1])
+        elif name == "side":
             _, off, q, axis, d = step
             wait(("side", off, q))
             slot = ((z + off[0]) % 4) * 4 + (y + off[1]) % 4
@@ -217,7 +256,8 @@
             dest = {"a": place(z, y, xa, core), "b": place(z, y, xb, core), "sib": sib}[to]
             remote(src, half_at(line_all, slot, half), 4, line_recv.at[slot, half], dest).start()
         elif name == "hub":
-            _, kb, zz = step
+            _, kb, dz = step
+            zz = (z + dz) % 4
 
             @pl.when(hub)
             def _():
@@ -227,7 +267,8 @@
                 low_send(yy, zz, kb, 5, place(z, y, xa, core))
                 low_send(yy, zz, kb, 6, sib)
         elif name == "p":
-            _, kb, zz = step
+            _, kb, dz = step
+            zz = (z + dz) % 4
             yy = 2 * (xb % 2) + core
 
             @pl.when(jnp.logical_not(hub))
@@ -236,8 +277,9 @@
                 low_send(yy, zz, kb, 5, place(z, y, xa, core))
                 low_send(yy, zz, kb, 6, sib)
         elif name == "q":
-            _, kb, zz = step
-            wait(("q", kb, zz))
+            _, kb, dz = step
+            zz = (z + dz) % 4
+            wait(("q", kb, dz))
             low_send(2 * (1 - xh % 2) + core, zz, kb, 6, sib)
         elif name == "far":
             _, kb, d = step
@@ -344,9 +386,13 @@
     def pieces(n):
         return low_all.at[pl.ds(0, n // 4)] if n >= 4 else low_all.at[0, pl.ds(0, n)]
 
-    @pl.when(jnp.logical_not(side_self))
+    @pl.when(c != 0)
     def _():
         sent(side_all.at[0], 0)
+
+    @pl.when(r % 8 != 0)
+    def _():
+        sent(side_all.at[0], 9)
 
     @pl.when(hub)
     def _():
@@ -392,12 +438,13 @@
             pltpu.VMEM((2560, BLOCK), dt),
             pltpu.VMEM((2, BLOCK, 2048), dt),
             pltpu.VMEM((1024, 512), dt),
-            dma((4, 4, 4)), dma((16, 4)), dma((4, 2)), dma((8, 2)), dma((4, 2)), dma((4, 2)),
-            dma((9,)), dma((2,)), dma((4,)), dma((5,)),
+            pltpu.VMEM((1024, 512), dt),
+            dma((4, 4, 4)), dma((16, 4)), dma((4, 2)), dma((8, 2)), dma((4, 2)), dma((4, 2)), dma((4,)),
+            dma((10,)), dma((2,)), dma((4,)), dma((5,)),
         ],
         compiler_params=pltpu.CompilerParams(has_side_effects=True, vmem_limit_bytes=67043328),
         name="fused",
-    )(low, side.reshape(4, BLOCK, 512), grad)
+    )(low, side, grad)
 
 
 def per_device(low, side, grad):

time: 254 us -> 250 us (0.984)
  Pallas kernels: 246 us -> 242 us
    pallas_call x1, Pallas kernels: 246 us -> 242 us  [fused(): pl.pallas_call(kernel, out_shape=[jax.ShapeDtypeStruct(grad.shape, dt), j...]
where the time goes in v3:
time: 250 us; the launch traced here: 248 us
  Pallas kernels  242 us (97%)
  other arithmetic  4.34 us (2%)
    pallas_call x1, Pallas kernels, fused(): pl.pallas_call(kernel, out_shape=[jax.ShapeDtypeStruct(grad.shape, dt), j...  242 us

profile of v3, /device:TPU:1, one launch (start us, length us, event | category | flops | bytes accessed | tf_op | source)
XLA Modules:
  0.0 247.8 jit_solution(3812313103506907520)
XLA Ops:
  0.6 241.8 %fused.1 = (bf16[1024,512]{1,0:T(8,128)(2,1)}, bf16[1024,2048]{1,0:T(8,128)(2,1)}, bf16[4,4,2560,256]{3,2,1,0:T(8,128)(2,1)}) custom-call(bf16[1024,2048]{1,0:T(8,128)(2,1)} %low_ref.1, bf16[1024,512]{1,0:T(8,128)(2,1)} %side_ref.1, bf16[1024,512]{1,0:T(8,128)(2,1)} %grad_ref.1), custom_call_target="tpu_custom_call" | custom-call | tf_op jit(solution)/shard_map/fused/pallas_call | solution.py:423
  242.5 0.0 copy-start
  242.5 4.3 %compare_select_fusion = bf16[1024,2048]{1,0:T(8,128)(2,1)} fusion(bf16[1024,2048]{1,0:T(8,128)(2,1)} %get-tuple-element.5, s32[2048]{0:T(1024)S(1)} %fusion.9, s32[1024]{0:T(1024)S(1)} %fusion.20), kind=kLoop, calls=%fused_computation | loop fusion | flops 4194304 | bytes 8400896 | tf_op jit(solution)/shard_map/jit(_where)/select_n | solution.py:456
  246.8 0.0 copy-done
  246.8 1.0 copy.6
  (2 shorter events, 0.0 us)
Async XLA Ops:
  242.5 4.3 %copy-start = (bf16[1024,512]{1,0:T(8,128)(2,1)S(1)}, bf16[1024,512]{1,0:T(8,128)(2,1)}, u32[]{:S(2)}) copy-start(bf16[1024,512]{1,0:T(8,128)(2,1)} %get-tuple-element.8) | copy-start | bytes 3145732

commit v4 on v3

--- a/solution.py
+++ b/solution.py
@@ -9,6 +9,7 @@
 MESH = pl.DeviceIdType.MESH
 NROWS = (1024, 768, 512, 256)
 FIRST = (0, 1024, 1792, 2304)
+ORDER = (3, 1, 0, 2)
 LAG = 2.5
 
 
@@ -24,8 +25,10 @@
             moved = list(off)
             moved[axis] = (moved[axis] - d) % 4
             return tuple(moved)
-        ready[("mid", q)] = 8.0 + 6.0 * q
-        job(("mid", q), "spread", 6.0, ("side", (0, 0), q), 0, ("spread", q))
+        ready[("mid", q)] = 16.0 + 8.0 * q
+        job(("mid", q), "spread", 8.0, ("side", (0, 0), q), 0, ("spread", q))
+        job(("mid", q), "a", 5.65, ("spread a", q), 0, ("none",))
+        job(("mid", q), "b", 5.65, ("spread b", q), 0, ("none",))
         for lane in (None, 0, 1, 3, 2):
             axis = first if lane is None else 1 - first
             own = [0, 0]
@@ -38,29 +41,30 @@
             d = 1 if q % 2 == 0 else -1
             near = hop(own, axis, d)
             job(("side", near, q), ("zy"[axis], d), 5.65, ("side", hop(near, axis, d), q), prio, ("side", near, q, axis, d))
-    for half in range(2):
+    for half in (1, 0):
         ready[("grad", 0, half)] = 0.0
-        ready[("line", "own", half)] = 0.0
+        ready[("line", "own", half)] = 110.0 * (1 - half)
         for d in (1, -1):
-            job(("grad", 0, half), ("z", d), 11.3, ("grad", -d % 4, half), 3, ("grad", 0, half, d))
+            job(("grad", 0, half), ("z", d), 11.3, ("grad", -d % 4, half), 2 - half, ("grad", 0, half, d))
         d = 1 if half == 0 else -1
-        job(("grad", -d % 4, half), ("z", d), 11.3, ("grad", 2, half), 3, ("grad", -d % 4, half, d))
+        job(("grad", -d % 4, half), ("z", d), 11.3, ("grad", 2, half), 2 - half, ("grad", -d % 4, half, d))
         for to in "ab":
             job(("line", "own", half), to, 11.3, ("line", to, half), 4, ("line", "own", half, to))
         src, to = ("a", "b") if half == 0 else ("b", "a")
         job(("line", src, half), to, 11.3, ("line", "o", half), 4, ("line", src, half, to))
         for piece in ("own", "a", "b", "o"):
             job(("line", piece, half), "sib", 1.0, ("line", piece + "s", half), 4, ("line", piece, half, "sib"))
-    ready[("move", 0)] = 0.0
-    for kb in range(4):
+    ready[("move", ORDER[0])] = 0.0
+    ready[("hub", "end", 0)] = 0.0
+    for n, kb in enumerate(ORDER):
         cost = 11.3 * NROWS[kb] / 1024
         for d in (1, -1):
-            job(("move", kb), ("z", d), 1.5 * cost, ("move", kb + 1) if d == 1 else ("moved", kb), (0, 0, 4, 4)[kb], ("move", kb, d))
+            job(("move", kb), ("z", d), 1.5 * cost, ("move", (ORDER + ("end",))[n + 1]) if d == 1 else ("moved", kb), (0, 0, 0.5, 1.5)[n], ("move", kb, d))
         for zz in range(4):
-            job(("hub", kb, zz), "b", cost, ("p", kb, zz), 2 + 0.1 * kb, ("hub", kb, zz))
-            job(("p", kb, zz), "a", cost, ("q", kb, zz), 2 + 0.1 * kb, ("p", kb, zz))
+            job(("hub", kb, zz), "b", cost, ("p", kb, zz), 2 + 0.1 * n, ("hub", kb, zz))
+            job(("p", kb, zz), "a", cost, ("q", kb, zz), 2 + 0.1 * n, ("p", kb, zz))
             job(("q", kb, zz), "sib", 0.1 * cost, ("qs", kb, zz), 2, ("q", kb, zz))
-        ready[("hub", kb, 0)] = 4.0 + kb
+        ready[("hub", kb, 0)] = 4.0 + n
     free = {}
     pending = list(jobs)
     while pending:
@@ -76,19 +80,18 @@
             for zz, extra in ((1, 0.0), (3, 0.0), (2, cost / 3)):
                 ready[("hub", step[1], zz)] = start + cost + LAG + extra
         steps.append((max(ready[need], start - 12.0), start, ("send",) + step))
-        for kb in range(4):
+        for kb in ORDER:
             key = ("sum", kb)
-            if key not in ready and all(("qs", kb, zz) in ready for zz in range(4)) and ("grad", 2, 0) in ready and ("grad", 2, 1) in ready:
-                now = max(t for e, t in ready.items() if e[:2] == ("qs", kb) or e[0] == "grad") + 3.0
+            if key not in ready and all(("qs", kb, zz) in ready for zz in range(4)) and ("grad", 2, 1) in ready and (kb > 1 or ("grad", 2, 0) in ready):
+                now = max(t for e, t in ready.items() if e[:2] == ("qs", kb) or e[0] == "grad" and (kb < 2 or e[2] == 1)) + 3.0
                 ready[key] = now
                 steps.append((now, now, ("part", kb)))
                 for d in (1, -1):
-                    pending.append((key, ("y", d), 5.65, ("hop", kb, d), 0, ("far", kb, d)))
+                    pending.append((key, ("y", d), 5.65, ("hop", kb, d), 0, ("none",)))
                     pending.append((("hop", kb, d), ("y", d), 11.3, ("got", kb, d), 0, ("near", kb, d)))
-    slots = sorted((max(ready[("side", (a, b), q)] for q in range(4)), (a, b)) for a in range(4) for b in range(4))
     for g in range(4):
-        steps.append((1e4 + (g // 2) * 10, g, ("dot", tuple(off for _, off in slots[4 * g:4 * g + 4]))))
-    steps = [(1e4 + 5, b, s) if s[:3] == ("send", "near", 3) else (a, b, s) for a, b, s in steps]
+        steps.append((1e4 + (g // 2) * 10, g, ("dot", ("own", "a", "b", "o")[g])))
+    steps = [(1e4 + 5, b, s) if s[:3] == ("send", "near", ORDER[-1]) else (a, b, s) for a, b, s in steps]
     steps.sort(key=lambda t: (t[0], t[1]))
     return [s for _, _, s in steps], ready
 
@@ -102,9 +105,6 @@
     xa, xb = x + 1 - 2 * (x % 2), 3 - x
     xh = jnp.where(hub, x, xb)
 
-    def bxor(a, b):
-        return sum(((a // n % 2 + b // n % 2) % 2) * n for n in (1, 2, 4))
-
     def place(zz, yy, xx, cc):
         return {"row": zz * 4 + yy, "col": xx * 2 + cc}
 
@@ -117,37 +117,52 @@
     sib = place(z, y, x, 1 - core)
     up, down = place(z, (y + 1) % 4, x, core), place(z, (y + 3) % 4, x, core)
 
-    turn = bxor(c, r % 8)
-    side_row = (r // 8) * 8 + turn
+    def shift(sig, kk):
+        return (sig + kk * (5 - 2 * sig)) % 4
+
+    def spread_row(cj, cc):
+        return 2 * shift((cc // 2 + 4 - cj // 2) % 4, cj % 2) + (cj + cc) % 2
+
+    def spread_col(row8, cj):
+        return 2 * ((cj // 2 + shift(row8 // 2, cj % 2)) % 4) + (cj + row8) % 2
+
+    def spread_from(row8, cc):
+        kk = (cc + row8) % 2
+        return 2 * ((cc // 2 + 4 - shift(row8 // 2, kk)) % 4) + kk
+
+    side_row = (r // 8) * 8 + spread_row(c, r % 8)
+    side_col = spread_col(r % 8, c)
+    stays, direct = side_row == r, c == r % 8
 
     def quarter(ref, q):
         return ref.at[pl.ds(q * BLOCK, BLOCK)]
 
-    @pl.when((c != 0) & (turn != 0))
-    def _():
-        for q in range(4):
-            remote(quarter(side_ref, q), quarter(mid, q), 0, mid_recv.at[q], {"row": side_row, "col": c}).start()
-
-    @pl.when((c != 0) & (turn == 0))
-    def _():
-        for q in range(4):
-            remote(quarter(side_ref, q), quarter(side_all.at[side_row], q), 0, side_recv.at[side_row, q],
-                   {"row": side_row, "col": c}).start()
-
-    @pl.when((c == 0) & (turn == 0))
-    def _():
-        for q in range(4):
-            pltpu.make_async_copy(quarter(side_ref, q), quarter(side_all.at[r], q), side_recv.at[r, q]).start()
+    def spread_first():
+        @pl.when(jnp.logical_not(stays) & jnp.logical_not(direct))
+        def _():
+            for q in range(4):
+                remote(quarter(side_ref, q), quarter(mid, q), 0, mid_recv.at[q], {"row": side_row, "col": c}).start()
+
+        @pl.when(jnp.logical_not(stays) & direct)
+        def _():
+            for q in range(4):
+                remote(quarter(side_ref, q), quarter(side_all.at[side_row], q), 0, side_recv.at[side_row, q],
+                       {"row": side_row, "col": c}).start()
+
+        @pl.when(stays & direct)
+        def _():
+            for q in range(4):
+                pltpu.make_async_copy(quarter(side_ref, q), quarter(side_all.at[r], q), side_recv.at[r, q]).start()
 
     def spread(q):
-        to = {"row": r, "col": turn}
-
-        @pl.when((r % 8 != 0) & (c != 0))
+        to = {"row": r, "col": side_col}
+
+        @pl.when((side_col != c) & (side_col != r % 8))
         def _():
             arrive(quarter(mid, q), mid_recv.at[q])
             remote(quarter(mid, q), quarter(side_all.at[r], q), 9, side_recv.at[r, q], to).start()
 
-        @pl.when((r % 8 != 0) & (c == 0))
+        @pl.when((side_col != c) & (side_col == r % 8))
         def _():
             remote(quarter(side_ref, q), quarter(side_all.at[r], q), 9, side_recv.at[r, q], to).start()
 
@@ -166,7 +181,7 @@
 
     @pl.when(hub)
     def _():
-        for kb in range(4):
+        for kb in ORDER:
             pltpu.make_async_copy(low_piece(here, kb), stage_at(kb), stage_sem.at[kb]).start()
 
     def move(kb):
@@ -181,7 +196,9 @@
                 remote(low_piece(h, kb), low_at(mine, z, kb), 1, low_recv.at[mine, z, kb],
                        place(x // 2 + 2 * h, y, x, core)).start()
 
-    move(0)
+    move(ORDER[0])
+    move(ORDER[1])
+    spread_first()
 
     own_grad = pltpu.make_async_copy(grad_ref, grad_all.at[z], out_sem.at[0])
     own_line = pltpu.make_async_copy(grad_ref, line_all.at[c], out_sem.at[1])
@@ -190,7 +207,7 @@
 
     @pl.when(hub)
     def _():
-        for kb in range(4):
+        for kb in ORDER:
             pltpu.make_async_copy(low_piece(here, kb), stage_at(kb), stage_sem.at[kb]).wait()
             pltpu.make_async_copy(stage_at(kb), low_at(mine, z, kb), low_recv.at[mine, z, kb]).start()
 
@@ -231,7 +248,7 @@
         if name == "spread":
             spread(step[1])
         elif name == "move":
-            if step[1] and step[2] == 1:
+            if step[1] in ORDER[2:] and step[2] == 1:
                 move(step[1])
         elif name == "side":
             _, off, q, axis, d = step
@@ -298,11 +315,11 @@
         for zz in range(4):
             for name in ("ps", "q", "qs"):
                 wait((name, kb, zz))
-        if kb == 0:
+        if kb == ORDER[0]:
             own_grad.wait()
-            for off in (1, 2, 3):
-                for half in range(2):
-                    wait(("grad", off, half))
+        for off in (1, 2, 3):
+            for half in (1,) if kb > 1 else (0, 1):
+                wait(("grad", off, half))
         n = NROWS[kb]
 
         def load(t):
@@ -323,33 +340,37 @@
             part[kb, t] = total
             return carry
 
-        lax.fori_loop(0, 4, body, 0)
-
-    def add_dot(offs, start):
+        body(0, 0)
+        send(("far", kb, 1))
+        send(("far", kb, -1))
+        lax.fori_loop(1, 4, body, 0)
+
+    def add_dot(piece, start):
+        for name in (piece, piece + "s"):
+            if name != "own":
+                for half in range(2):
+                    wait(("line", name, half))
         if start:
             own_line.wait()
-            for piece in ("a", "b", "o", "owns", "as", "bs", "os"):
-                for half in range(2):
-                    wait(("line", piece, half))
-            acc[...] = jnp.zeros_like(acc)
-        slots = []
-        for off in offs:
-            for q in range(4):
-                wait(("side", off, q))
-            slots.append(((z + off[0]) % 4) * 4 + (y + off[1]) % 4)
+            for a in range(4):
+                for b in range(4):
+                    for q in range(4):
+                        wait(("side", (a, b), q))
+        first = line_slot(piece) // 2
 
         def body(i, carry):
-            slot = slots[3]
-            for n in range(3):
-                slot = jnp.where(i == n, slots[n], slot)
-            h, cj = slot // 8, bxor(slot % 8, c)
+            cj = 2 * first + i % 2
+            h = i // 2
+            slot = 8 * h + spread_row(cj, c)
             for bi in range(4):
                 n = (bi + 1) * BLOCK
-                acc[h, bi, :, :n] += lax.dot_general(
-                    line_all[cj, bi * BLOCK:(bi + 1) * BLOCK], side_all[slot, :n],
-                    (((1,), (1,)), ((), ())), preferred_element_type=jnp.float32)
+                total = lax.dot_general(line_all[cj, bi * BLOCK:(bi + 1) * BLOCK], side_all[slot, :n],
+                                        (((1,), (1,)), ((), ())), preferred_element_type=jnp.float32)
+                acc[h, bi, :, :n] += total
             return carry
 
+        if start:
+            acc[...] = jnp.zeros_like(acc)
         lax.fori_loop(0, 4, body, 0)
 
     started = False
@@ -386,11 +407,11 @@
     def pieces(n):
         return low_all.at[pl.ds(0, n // 4)] if n >= 4 else low_all.at[0, pl.ds(0, n)]
 
-    @pl.when(c != 0)
+    @pl.when(jnp.logical_not(stays))
     def _():
         sent(side_all.at[0], 0)
 
-    @pl.when(r % 8 != 0)
+    @pl.when(side_col != c)
     def _():
         sent(side_all.at[0], 9)
 

time: 250 us -> 252 us (level)
  the two profiles are of different devices: /device:TPU:1 before, /device:TPU:37 now
where the time goes in v4:
time: 252 us
  Pallas kernels  246 us (98%)
  other arithmetic  4.34 us (2%)
    pallas_call x1, Pallas kernels, fused(): pl.pallas_call(kernel, out_shape=[jax.ShapeDtypeStruct(grad.shape, dt), j...  246 us

profile of v4, /device:TPU:37, one launch (start us, length us, event | category | flops | bytes accessed | tf_op | source)
XLA Modules:
  0.0 251.8 jit_solution(17925567711783125640)
XLA Ops:
  0.6 245.9 %fused.1 = (bf16[1024,512]{1,0:T(8,128)(2,1)}, bf16[1024,2048]{1,0:T(8,128)(2,1)}, bf16[4,4,2560,256]{3,2,1,0:T(8,128)(2,1)}) custom-call(bf16[1024,2048]{1,0:T(8,128)(2,1)} %low_ref.1, bf16[1024,512]{1,0:T(8,128)(2,1)} %side_ref.1, bf16[1024,512]{1,0:T(8,128)(2,1)} %grad_ref.1), custom_call_target="tpu_custom_call" | custom-call | tf_op jit(solution)/shard_map/fused/pallas_call | solution.py:444
  246.5 0.0 copy-start
  246.5 4.3 %compare_select_fusion = bf16[1024,2048]{1,0:T(8,128)(2,1)} fusion(bf16[1024,2048]{1,0:T(8,128)(2,1)} %get-tuple-element.5, s32[2048]{0:T(1024)S(1)} %fusion.9, s32[1024]{0:T(1024)S(1)} %fusion.20), kind=kLoop, calls=%fused_computation | loop fusion | flops 4194304 | bytes 8400896 | tf_op jit(solution)/shard_map/jit(_where)/select_n | solution.py:477
  250.9 0.0 copy-done
  250.9 1.0 copy.6
  (2 shorter events, 0.0 us)
Async XLA Ops:
  246.5 4.3 %copy-start = (bf16[1024,512]{1,0:T(8,128)(2,1)S(1)}, bf16[1024,512]{1,0:T(8,128)(2,1)}, u32[]{:S(2)}) copy-start(bf16[1024,512]{1,0:T(8,128)(2,1)} %get-tuple-element.8) | copy-start | bytes 3145732

commit v5 on v4

--- a/solution.py
+++ b/solution.py
@@ -10,6 +10,7 @@
 NROWS = (1024, 768, 512, 256)
 FIRST = (0, 1024, 1792, 2304)
 ORDER = (3, 1, 0, 2)
+SLACK = 5.0
 LAG = 2.5
 
 
@@ -27,8 +28,8 @@
             return tuple(moved)
         ready[("mid", q)] = 16.0 + 8.0 * q
         job(("mid", q), "spread", 8.0, ("side", (0, 0), q), 0, ("spread", q))
-        job(("mid", q), "a", 5.65, ("spread a", q), 0, ("none",))
-        job(("mid", q), "b", 5.65, ("spread b", q), 0, ("none",))
+        job(("mid", q), "a", 2.8, ("spread a", q), 0, ("none",))
+        job(("mid", q), "b", 2.8, ("spread b", q), 0, ("none",))
         for lane in (None, 0, 1, 3, 2):
             axis = first if lane is None else 1 - first
             own = [0, 0]
@@ -43,15 +44,15 @@
             job(("side", near, q), ("zy"[axis], d), 5.65, ("side", hop(near, axis, d), q), prio, ("side", near, q, axis, d))
     for half in (1, 0):
         ready[("grad", 0, half)] = 0.0
-        ready[("line", "own", half)] = 110.0 * (1 - half)
+        ready[("line", "own", half)] = 0.0
         for d in (1, -1):
             job(("grad", 0, half), ("z", d), 11.3, ("grad", -d % 4, half), 2 - half, ("grad", 0, half, d))
         d = 1 if half == 0 else -1
         job(("grad", -d % 4, half), ("z", d), 11.3, ("grad", 2, half), 2 - half, ("grad", -d % 4, half, d))
         for to in "ab":
-            job(("line", "own", half), to, 11.3, ("line", to, half), 4, ("line", "own", half, to))
-        src, to = ("a", "b") if half == 0 else ("b", "a")
-        job(("line", src, half), to, 11.3, ("line", "o", half), 4, ("line", src, half, to))
+            job(("line", "own", half), to, 11.3, ("line", to, half), 1, ("line", "own", half, to))
+        job(("late", "a", half), "b", 11.3, ("line", "o", half), 4, ("line", "a", half, "b"))
+        ready[("late", "a", half)] = 130.0
         for piece in ("own", "a", "b", "o"):
             job(("line", piece, half), "sib", 1.0, ("line", piece + "s", half), 4, ("line", piece, half, "sib"))
     ready[("move", ORDER[0])] = 0.0
@@ -64,7 +65,8 @@
             job(("hub", kb, zz), "b", cost, ("p", kb, zz), 2 + 0.1 * n, ("hub", kb, zz))
             job(("p", kb, zz), "a", cost, ("q", kb, zz), 2 + 0.1 * n, ("p", kb, zz))
             job(("q", kb, zz), "sib", 0.1 * cost, ("qs", kb, zz), 2, ("q", kb, zz))
-        ready[("hub", kb, 0)] = 4.0 + n
+        ready[("hub", kb, 0)] = 6.0 + 2 * n
+        steps.append((2.0 + 2 * n, n, ("send", "stage", kb)))
     free = {}
     pending = list(jobs)
     while pending:
@@ -79,7 +81,9 @@
             ready[made] = start + cost
             for zz, extra in ((1, 0.0), (3, 0.0), (2, cost / 3)):
                 ready[("hub", step[1], zz)] = start + cost + LAG + extra
-        steps.append((max(ready[need], start - 12.0), start, ("send",) + step))
+        lazy = SLACK if step[0] == "side" and step[1] != (0, 0) else 0.0
+        late = 1e4 + 11 if step[:2] == ("line", "o") else 0.0
+        steps.append((max(ready[need] + lazy, start - 12.0, late), start, ("send",) + step))
         for kb in ORDER:
             key = ("sum", kb)
             if key not in ready and all(("qs", kb, zz) in ready for zz in range(4)) and ("grad", 2, 1) in ready and (kb > 1 or ("grad", 2, 0) in ready):
@@ -90,7 +94,7 @@
                     pending.append((key, ("y", d), 5.65, ("hop", kb, d), 0, ("none",)))
                     pending.append((("hop", kb, d), ("y", d), 11.3, ("got", kb, d), 0, ("near", kb, d)))
     for g in range(4):
-        steps.append((1e4 + (g // 2) * 10, g, ("dot", ("own", "a", "b", "o")[g])))
+        steps.append((1e4 + (0, 10, 12, 13)[g], g, ("dot", ("own", "a", "b", "o")[g])))
     steps = [(1e4 + 5, b, s) if s[:3] == ("send", "near", ORDER[-1]) else (a, b, s) for a, b, s in steps]
     steps.sort(key=lambda t: (t[0], t[1]))
     return [s for _, _, s in steps], ready
@@ -205,9 +209,11 @@
     own_grad.start()
     own_line.start()
 
-    @pl.when(hub)
-    def _():
-        for kb in ORDER:
+    acc[...] = jnp.zeros_like(acc)
+
+    def put_stage(kb):
+        @pl.when(hub)
+        def _():
             pltpu.make_async_copy(low_piece(here, kb), stage_at(kb), stage_sem.at[kb]).wait()
             pltpu.make_async_copy(stage_at(kb), low_at(mine, z, kb), low_recv.at[mine, z, kb]).start()
 
@@ -247,6 +253,8 @@
         name = step[0]
         if name == "spread":
             spread(step[1])
+        elif name == "stage":
+            put_stage(step[1])
         elif name == "move":
             if step[1] in ORDER[2:] and step[2] == 1:
                 move(step[1])
@@ -369,8 +377,6 @@
                 acc[h, bi, :, :n] += total
             return carry
 
-        if start:
-            acc[...] = jnp.zeros_like(acc)
         lax.fori_loop(0, 4, body, 0)
 
     started = False

time: 252 us -> 229 us (0.909)
  the two profiles are of different devices: /device:TPU:37 before, /device:TPU:32 now
where the time goes in v5:
time: 229 us
  Pallas kernels  223 us (97%)
  other arithmetic  4.34 us (2%)
    pallas_call x1, Pallas kernels, fused(): pl.pallas_call(kernel, out_shape=[jax.ShapeDtypeStruct(grad.shape, dt), j...  223 us

profile of v5, /device:TPU:32, one launch (start us, length us, event | category | flops | bytes accessed | tf_op | source)
XLA Modules:
  0.0 228.8 jit_solution(1082724973842964719)
XLA Ops:
  0.6 222.9 %fused.1 = (bf16[1024,512]{1,0:T(8,128)(2,1)}, bf16[1024,2048]{1,0:T(8,128)(2,1)}, bf16[4,4,2560,256]{3,2,1,0:T(8,128)(2,1)}) custom-call(bf16[1024,2048]{1,0:T(8,128)(2,1)} %low_ref.1, bf16[1024,512]{1,0:T(8,128)(2,1)} %side_ref.1, bf16[1024,512]{1,0:T(8,128)(2,1)} %grad_ref.1), custom_call_target="tpu_custom_call" | custom-call | tf_op jit(solution)/shard_map/fused/pallas_call | solution.py:450
  223.5 0.0 copy-start
  223.5 4.3 %compare_select_fusion = bf16[1024,2048]{1,0:T(8,128)(2,1)} fusion(bf16[1024,2048]{1,0:T(8,128)(2,1)} %get-tuple-element.5, s32[2048]{0:T(1024)S(1)} %fusion.9, s32[1024]{0:T(1024)S(1)} %fusion.20), kind=kLoop, calls=%fused_computation | loop fusion | flops 4194304 | bytes 8400896 | tf_op jit(solution)/shard_map/jit(_where)/select_n | solution.py:483
  227.9 0.0 copy-done
  227.9 1.0 copy.6
  (2 shorter events, 0.0 us)
Async XLA Ops:
  223.5 4.3 %copy-start = (bf16[1024,512]{1,0:T(8,128)(2,1)S(1)}, bf16[1024,512]{1,0:T(8,128)(2,1)}, u32[]{:S(2)}) copy-start(bf16[1024,512]{1,0:T(8,128)(2,1)} %get-tuple-element.8) | copy-start | bytes 3145732

commit v6 on v5

--- a/solution.py
+++ b/solution.py
@@ -11,6 +11,9 @@
 FIRST = (0, 1024, 1792, 2304)
 ORDER = (3, 1, 0, 2)
 SLACK = 5.0
+QROWS = (288, 288, 224, 224)
+QFIRST = (0, 288, 576, 800)
+LINE = 100.0
 LAG = 2.5
 
 
@@ -22,6 +25,7 @@
 
     for q in range(4):
         first = 1 if q < 2 else 0
+        cost = 11.3 * QROWS[q] / 512
         def hop(off, axis, d):
             moved = list(off)
             moved[axis] = (moved[axis] - d) % 4
@@ -38,19 +42,19 @@
             own = tuple(own)
             prio = 1 if lane is None else 5
             for d in (1, -1):
-                job(("side", own, q), ("zy"[axis], d), 5.65, ("side", hop(own, axis, d), q), prio, ("side", own, q, axis, d))
+                job(("side", own, q), ("zy"[axis], d), cost, ("side", hop(own, axis, d), q), prio, ("side", own, q, axis, d))
             d = 1 if q % 2 == 0 else -1
             near = hop(own, axis, d)
-            job(("side", near, q), ("zy"[axis], d), 5.65, ("side", hop(near, axis, d), q), prio, ("side", near, q, axis, d))
+            job(("side", near, q), ("zy"[axis], d), cost, ("side", hop(near, axis, d), q), prio, ("side", near, q, axis, d))
     for half in (1, 0):
         ready[("grad", 0, half)] = 0.0
-        ready[("line", "own", half)] = 0.0
+        ready[("line", "own", half)] = LINE
         for d in (1, -1):
-            job(("grad", 0, half), ("z", d), 11.3, ("grad", -d % 4, half), 2 - half, ("grad", 0, half, d))
+            job(("grad", 0, half), ("z", d), 11.3, ("grad", -d % 4, half), 1.2 if half == 0 else 1, ("grad", 0, half, d))
         d = 1 if half == 0 else -1
-        job(("grad", -d % 4, half), ("z", d), 11.3, ("grad", 2, half), 2 - half, ("grad", -d % 4, half, d))
+        job(("grad", -d % 4, half), ("z", d), 11.3, ("grad", 2, half), 1.2 if half == 0 else 1, ("grad", -d % 4, half, d))
         for to in "ab":
-            job(("line", "own", half), to, 11.3, ("line", to, half), 1, ("line", "own", half, to))
+            job(("line", "own", half), to, 11.3, ("line", to, half), 4, ("line", "own", half, to))
         job(("late", "a", half), "b", 11.3, ("line", "o", half), 4, ("line", "a", half, "b"))
         ready[("late", "a", half)] = 130.0
         for piece in ("own", "a", "b", "o"):
@@ -67,6 +71,7 @@
             job(("q", kb, zz), "sib", 0.1 * cost, ("qs", kb, zz), 2, ("q", kb, zz))
         ready[("hub", kb, 0)] = 6.0 + 2 * n
         steps.append((2.0 + 2 * n, n, ("send", "stage", kb)))
+    steps.append((28.0, 0, ("send", "zero")))
     free = {}
     pending = list(jobs)
     while pending:
@@ -82,7 +87,9 @@
             for zz, extra in ((1, 0.0), (3, 0.0), (2, cost / 3)):
                 ready[("hub", step[1], zz)] = start + cost + LAG + extra
         lazy = SLACK if step[0] == "side" and step[1] != (0, 0) else 0.0
-        late = 1e4 + 11 if step[:2] == ("line", "o") else 0.0
+        late = 0.0
+        if step[0] == "line" and step[-1] == "sib":
+            late = {"own": 120.0, "o": 1e4 + 11}.get(step[1], 1e4 + 8)
         steps.append((max(ready[need] + lazy, start - 12.0, late), start, ("send",) + step))
         for kb in ORDER:
             key = ("sum", kb)
@@ -94,8 +101,7 @@
                     pending.append((key, ("y", d), 5.65, ("hop", kb, d), 0, ("none",)))
                     pending.append((("hop", kb, d), ("y", d), 11.3, ("got", kb, d), 0, ("near", kb, d)))
     for g in range(4):
-        steps.append((1e4 + (0, 10, 12, 13)[g], g, ("dot", ("own", "a", "b", "o")[g])))
-    steps = [(1e4 + 5, b, s) if s[:3] == ("send", "near", ORDER[-1]) else (a, b, s) for a, b, s in steps]
+        steps.append((1e4 + (7, 10, 12, 13)[g], g, ("dot", ("own", "a", "b", "o")[g])))
     steps.sort(key=lambda t: (t[0], t[1]))
     return [s for _, _, s in steps], ready
 
@@ -139,7 +145,7 @@
     stays, direct = side_row == r, c == r % 8
 
     def quarter(ref, q):
-        return ref.at[pl.ds(q * BLOCK, BLOCK)]
+        return ref.at[pl.ds(QFIRST[q], QROWS[q])]
 
     def spread_first():
         @pl.when(jnp.logical_not(stays) & jnp.logical_not(direct))
@@ -208,8 +214,6 @@
     own_line = pltpu.make_async_copy(grad_ref, line_all.at[c], out_sem.at[1])
     own_grad.start()
     own_line.start()
-
-    acc[...] = jnp.zeros_like(acc)
 
     def put_stage(kb):
         @pl.when(hub)
@@ -234,7 +238,7 @@
         name = event[0]
         if name == "side":
             slot = ((z + event[1][0]) % 4) * 4 + (y + event[1][1]) % 4
-            arrive(side_all.at[slot, pl.ds(event[2] * BLOCK, BLOCK)], side_recv.at[slot, event[2]])
+            arrive(quarter(side_all.at[slot], event[2]), side_recv.at[slot, event[2]])
         elif name == "grad":
             slot = (z + event[1]) % 4
             arrive(half_at(grad_all, slot, event[2]), grad_recv.at[slot, event[2]])
@@ -255,6 +259,8 @@
             spread(step[1])
         elif name == "stage":
             put_stage(step[1])
+        elif name == "zero":
+            acc[...] = jnp.zeros_like(acc)
         elif name == "move":
             if step[1] in ORDER[2:] and step[2] == 1:
                 move(step[1])
@@ -263,7 +269,7 @@
             wait(("side", off, q))
             slot = ((z + off[0]) % 4) * 4 + (y + off[1]) % 4
             to = place((z + d + 4) % 4, y, x, core) if axis == 0 else place(z, (y + d + 4) % 4, x, core)
-            ref = side_all.at[slot, pl.ds(q * BLOCK, BLOCK)]
+            ref = quarter(side_all.at[slot], q)
             remote(ref, ref, 2, side_recv.at[slot, q], to).start()
         elif name == "grad":
             _, off, half, d = step

time: 229 us -> 246 us (1.074)
  the two profiles are of different devices: /device:TPU:32 before, /device:TPU:33 now
where the time goes in v6:
time: 246 us
  Pallas kernels  240 us (98%)
  other arithmetic  4.34 us (2%)
    pallas_call x1, Pallas kernels, fused(): pl.pallas_call(kernel, out_shape=[jax.ShapeDtypeStruct(grad.shape, dt), j...  240 us

profile of v6, /device:TPU:33, one launch (start us, length us, event | category | flops | bytes accessed | tf_op | source)
XLA Modules:
  0.0 246.0 jit_solution(9466617007078654051)
XLA Ops:
  0.6 240.0 %fused.1 = (bf16[1024,512]{1,0:T(8,128)(2,1)}, bf16[1024,2048]{1,0:T(8,128)(2,1)}, bf16[4,4,2560,256]{3,2,1,0:T(8,128)(2,1)}) custom-call(bf16[1024,2048]{1,0:T(8,128)(2,1)} %low_ref.1, bf16[1024,512]{1,0:T(8,128)(2,1)} %side_ref.1, bf16[1024,512]{1,0:T(8,128)(2,1)} %grad_ref.1), custom_call_target="tpu_custom_call" | custom-call | tf_op jit(solution)/shard_map/fused/pallas_call | solution.py:456
  240.7 0.0 copy-start
  240.7 4.3 %compare_select_fusion = bf16[1024,2048]{1,0:T(8,128)(2,1)} fusion(bf16[1024,2048]{1,0:T(8,128)(2,1)} %get-tuple-element.5, s32[2048]{0:T(1024)S(1)} %fusion.9, s32[1024]{0:T(1024)S(1)} %fusion.20), kind=kLoop, calls=%fused_computation | loop fusion | flops 4194304 | bytes 8400896 | tf_op jit(solution)/shard_map/jit(_where)/select_n | solution.py:489
  245.0 0.0 copy-done
  245.0 1.0 copy.6
  (2 shorter events, 0.0 us)
Async XLA Ops:
  240.7 4.3 %copy-start = (bf16[1024,512]{1,0:T(8,128)(2,1)S(1)}, bf16[1024,512]{1,0:T(8,128)(2,1)}, u32[]{:S(2)}) copy-start(bf16[1024,512]{1,0:T(8,128)(2,1)} %get-tuple-element.8) | copy-start | bytes 3145732

commit v7 on v6

--- a/solution.py
+++ b/solution.py
@@ -13,7 +13,7 @@
 SLACK = 5.0
 QROWS = (288, 288, 224, 224)
 QFIRST = (0, 288, 576, 800)
-LINE = 100.0
+LINE = (110.0, 0.0)
 LAG = 2.5
 
 
@@ -48,7 +48,7 @@
             job(("side", near, q), ("zy"[axis], d), cost, ("side", hop(near, axis, d), q), prio, ("side", near, q, axis, d))
     for half in (1, 0):
         ready[("grad", 0, half)] = 0.0
-        ready[("line", "own", half)] = LINE
+        ready[("line", "own", half)] = LINE[half]
         for d in (1, -1):
             job(("grad", 0, half), ("z", d), 11.3, ("grad", -d % 4, half), 1.2 if half == 0 else 1, ("grad", 0, half, d))
         d = 1 if half == 0 else -1
@@ -56,7 +56,7 @@
         for to in "ab":
             job(("line", "own", half), to, 11.3, ("line", to, half), 4, ("line", "own", half, to))
         job(("late", "a", half), "b", 11.3, ("line", "o", half), 4, ("line", "a", half, "b"))
-        ready[("late", "a", half)] = 130.0
+        ready[("late", "a", half)] = 130.0 - 15.0 * half
         for piece in ("own", "a", "b", "o"):
             job(("line", piece, half), "sib", 1.0, ("line", piece + "s", half), 4, ("line", piece, half, "sib"))
     ready[("move", ORDER[0])] = 0.0
@@ -87,7 +87,7 @@
             for zz, extra in ((1, 0.0), (3, 0.0), (2, cost / 3)):
                 ready[("hub", step[1], zz)] = start + cost + LAG + extra
         lazy = SLACK if step[0] == "side" and step[1] != (0, 0) else 0.0
-        late = 0.0
+        late = 1e4 + 1 if step == ("line", "a", 0, "b") else 0.0
         if step[0] == "line" and step[-1] == "sib":
             late = {"own": 120.0, "o": 1e4 + 11}.get(step[1], 1e4 + 8)
         steps.append((max(ready[need] + lazy, start - 12.0, late), start, ("send",) + step))

time: 246 us -> 237 us (0.963)
  the two profiles are of different devices: /device:TPU:33 before, /device:TPU:102 now
where the time goes in v7:
time: 237 us; the launch traced here: 236 us
  Pallas kernels  230 us (97%)
  other arithmetic  4.34 us (2%)
    pallas_call x1, Pallas kernels, fused(): pl.pallas_call(kernel, out_shape=[jax.ShapeDtypeStruct(grad.shape, dt), j...  230 us

profile of v7, /device:TPU:102, one launch (start us, length us, event | category | flops | bytes accessed | tf_op | source)
XLA Modules:
  0.0 236.4 jit_solution(3103479474325719367)
XLA Ops:
  0.6 230.4 %fused.1 = (bf16[1024,512]{1,0:T(8,128)(2,1)}, bf16[1024,2048]{1,0:T(8,128)(2,1)}, bf16[4,4,2560,256]{3,2,1,0:T(8,128)(2,1)}) custom-call(bf16[1024,2048]{1,0:T(8,128)(2,1)} %low_ref.1, bf16[1024,512]{1,0:T(8,128)(2,1)} %side_ref.1, bf16[1024,512]{1,0:T(8,128)(2,1)} %grad_ref.1), custom_call_target="tpu_custom_call" | custom-call | tf_op jit(solution)/shard_map/fused/pallas_call | solution.py:456
  231.1 0.0 copy-start
  231.1 4.3 %compare_select_fusion = bf16[1024,2048]{1,0:T(8,128)(2,1)} fusion(bf16[1024,2048]{1,0:T(8,128)(2,1)} %get-tuple-element.5, s32[2048]{0:T(1024)S(1)} %fusion.9, s32[1024]{0:T(1024)S(1)} %fusion.20), kind=kLoop, calls=%fused_computation | loop fusion | flops 4194304 | bytes 8400896 | tf_op jit(solution)/shard_map/jit(_where)/select_n | solution.py:489
  235.4 0.0 copy-done
  235.4 1.0 copy.6
  (2 shorter events, 0.0 us)
Async XLA Ops:
  231.1 4.3 %copy-start = (bf16[1024,512]{1,0:T(8,128)(2,1)S(1)}, bf16[1024,512]{1,0:T(8,128)(2,1)}, u32[]{:S(2)}) copy-start(bf16[1024,512]{1,0:T(8,128)(2,1)} %get-tuple-element.8) | copy-start | bytes 3145732

commit v8 on v7

--- a/solution.py
+++ b/solution.py
@@ -10,10 +10,10 @@
 NROWS = (1024, 768, 512, 256)
 FIRST = (0, 1024, 1792, 2304)
 ORDER = (3, 1, 0, 2)
-SLACK = 5.0
-QROWS = (288, 288, 224, 224)
-QFIRST = (0, 288, 576, 800)
-LINE = (110.0, 0.0)
+SLACK = 0.0
+QROWS = (256, 256, 256, 256)
+QFIRST = (0, 256, 512, 768)
+LINE = (0.0, 0.0)
 LAG = 2.5
 
 
@@ -50,13 +50,13 @@
         ready[("grad", 0, half)] = 0.0
         ready[("line", "own", half)] = LINE[half]
         for d in (1, -1):
-            job(("grad", 0, half), ("z", d), 11.3, ("grad", -d % 4, half), 1.2 if half == 0 else 1, ("grad", 0, half, d))
+            job(("grad", 0, half), ("z", d), 11.3, ("grad", -d % 4, half), 2 if half == 0 else 1, ("grad", 0, half, d))
         d = 1 if half == 0 else -1
-        job(("grad", -d % 4, half), ("z", d), 11.3, ("grad", 2, half), 1.2 if half == 0 else 1, ("grad", -d % 4, half, d))
+        job(("grad", -d % 4, half), ("z", d), 11.3, ("grad", 2, half), 2 if half == 0 else 1, ("grad", -d % 4, half, d))
         for to in "ab":
-            job(("line", "own", half), to, 11.3, ("line", to, half), 4, ("line", "own", half, to))
+            job(("line", "own", half), to, 11.3, ("line", to, half), 1, ("line", "own", half, to))
         job(("late", "a", half), "b", 11.3, ("line", "o", half), 4, ("line", "a", half, "b"))
-        ready[("late", "a", half)] = 130.0 - 15.0 * half
+        ready[("late", "a", half)] = (130.0, 130.0)[half]
         for piece in ("own", "a", "b", "o"):
             job(("line", piece, half), "sib", 1.0, ("line", piece + "s", half), 4, ("line", piece, half, "sib"))
     ready[("move", ORDER[0])] = 0.0
@@ -87,10 +87,10 @@
             for zz, extra in ((1, 0.0), (3, 0.0), (2, cost / 3)):
                 ready[("hub", step[1], zz)] = start + cost + LAG + extra
         lazy = SLACK if step[0] == "side" and step[1] != (0, 0) else 0.0
-        late = 1e4 + 1 if step == ("line", "a", 0, "b") else 0.0
+        late = 0.0
         if step[0] == "line" and step[-1] == "sib":
-            late = {"own": 120.0, "o": 1e4 + 11}.get(step[1], 1e4 + 8)
-        steps.append((max(ready[need] + lazy, start - 12.0, late), start, ("send",) + step))
+            late = {"own": 0.0, "o": 1e4 + 11}.get(step[1], 0.0)
+        steps.append((max(ready[need] + lazy, start - 4.0, late), start, ("send",) + step))
         for kb in ORDER:
             key = ("sum", kb)
             if key not in ready and all(("qs", kb, zz) in ready for zz in range(4)) and ("grad", 2, 1) in ready and (kb > 1 or ("grad", 2, 0) in ready):
@@ -101,7 +101,8 @@
                     pending.append((key, ("y", d), 5.65, ("hop", kb, d), 0, ("none",)))
                     pending.append((("hop", kb, d), ("y", d), 11.3, ("got", kb, d), 0, ("near", kb, d)))
     for g in range(4):
-        steps.append((1e4 + (7, 10, 12, 13)[g], g, ("dot", ("own", "a", "b", "o")[g])))
+        steps.append((1e4 + (0, 10, 12, 13)[g], g, ("dot", ("own", "a", "b", "o")[g])))
+    steps = [(1e4 + 5, b, s) if s[:3] == ("send", "near", ORDER[-1]) else (a, b, s) for a, b, s in steps]
     steps.sort(key=lambda t: (t[0], t[1]))
     return [s for _, _, s in steps], ready
 

time: 237 us -> 226 us (0.954)
  the two profiles are of different devices: /device:TPU:102 before, /device:TPU:11 now
where the time goes in v8:
time: 226 us
  Pallas kernels  220 us (97%)
  other arithmetic  4.34 us (2%)
    pallas_call x1, Pallas kernels, fused(): pl.pallas_call(kernel, out_shape=[jax.ShapeDtypeStruct(grad.shape, dt), j...  220 us

profile of v8, /device:TPU:11, one launch (start us, length us, event | category | flops | bytes accessed | tf_op | source)
XLA Modules:
  0.0 226.0 jit_solution(17961878416403066987)
XLA Ops:
  0.6 220.1 %fused.1 = (bf16[1024,512]{1,0:T(8,128)(2,1)}, bf16[1024,2048]{1,0:T(8,128)(2,1)}, bf16[4,4,2560,256]{3,2,1,0:T(8,128)(2,1)}) custom-call(bf16[1024,2048]{1,0:T(8,128)(2,1)} %low_ref.1, bf16[1024,512]{1,0:T(8,128)(2,1)} %side_ref.1, bf16[1024,512]{1,0:T(8,128)(2,1)} %grad_ref.1), custom_call_target="tpu_custom_call" | custom-call | tf_op jit(solution)/shard_map/fused/pallas_call | solution.py:457
  220.7 0.0 copy-start
  220.7 4.3 %compare_select_fusion = bf16[1024,2048]{1,0:T(8,128)(2,1)} fusion(bf16[1024,2048]{1,0:T(8,128)(2,1)} %get-tuple-element.5, s32[2048]{0:T(1024)S(1)} %fusion.9, s32[1024]{0:T(1024)S(1)} %fusion.20), kind=kLoop, calls=%fused_computation | loop fusion | flops 4194304 | bytes 8400896 | tf_op jit(solution)/shard_map/jit(_where)/select_n | solution.py:490
  225.1 0.0 copy-done
  225.1 1.0 copy.6
  (2 shorter events, 0.0 us)
Async XLA Ops:
  220.7 4.3 %copy-start = (bf16[1024,512]{1,0:T(8,128)(2,1)S(1)}, bf16[1024,512]{1,0:T(8,128)(2,1)}, u32[]{:S(2)}) copy-start(bf16[1024,512]{1,0:T(8,128)(2,1)} %get-tuple-element.8) | copy-start | bytes 3145732
